TPU v7x, 32 devices: a whole 2x2x4 slice. The times are simulated.
32 devices in a mesh: grp: 8 (over z, x), tp: 4 (over y, core).
Axes of the slice: x: 2, y: 2, z: 4, core: 2. Of those that a mesh axis runs over, the one named last changes fastest.
Arguments:
- q_nope: bfloat16 [512, 16384], P('grp', 'tp'), may hold values from -6 to 6
- q_rope: bfloat16 [512, 8192], P('grp', 'tp'), may hold values from -500 to 500
- w_uk: bfloat16 [128, 128, 512], P('tp'), may hold values from -0.5 to 0.5
- w_uv: bfloat16 [128, 512, 128], P('tp'), may hold values from -1 to 1
- prefix_latent: bfloat16 [16, 2048, 512], P('grp'), may hold values from -5 to 5
- prefix_rope: bfloat16 [16, 64, 2048], P('grp'), may hold values from -8 to 8
- suffix_latent: bfloat16 [512, 256, 512], P(('grp', 'tp')), may hold values from -5 to 5
- suffix_rope: bfloat16 [512, 64, 256], P(('grp', 'tp')), may hold values from -4 to 4
- suffix_len: int32 [8, 64], P('grp'), may hold values from 1 to 256, 8192 in all within a row
- request_prefix: int32 [512], P('grp'), may hold values from 0 to 15, as said below
- prefix_slot: int32 [16], replicated, may hold values from 0 to 15, as said below
Outputs:
- attended: bfloat16 [512, 16384], P('grp', 'tp')
Inputs may be any that keep to these rules, and one draw needn't show every extreme that they name: `request_prefix`: of the requests of one group, at most 8 name the same prefix; in every draw one prefix is named by exactly 8 requests of every group. `prefix_slot`: A permutation: each cache row holds exactly one prefix. `suffix_len`: the lengths of one group sum to 8192, and one of them is 256.
All inputs are finite; a program needn't handle non-finite values.
Results may differ from a plain program's by a relative error of at most 0.018.
Values may be sent and summed in bfloat16 or wider, within the bound.
No kernel may reach another device: no remote copies, remote signals or barrier semaphores. Data moves between devices by JAX's collectives and lax.ppermute only.
A program may use at most 128 MiB of HBM per device.

v0:
```python
import functools
import math

import jax
import jax.numpy as jnp
from jax import lax
from jax.experimental import pallas as pl
from jax.experimental.pallas import tpu as pltpu
from jax.sharding import PartitionSpec as P


F32 = jnp.float32
BF16 = jnp.bfloat16
LANES = 128
NT = (((1,), (1,)), ((), ()))
TN = (((0,), (0,)), ((), ()))


def call(body, shapes, limit_mib, flops, scratch=(), scalars=(), far=(), args=()):
    spaces = [pltpu.SMEM] * len(scalars) + [pltpu.HBM] * len(far) + [pltpu.VMEM] * len(args)
    far = [pltpu.with_memory_space_constraint(x, pltpu.HBM) for x in far]
    return pl.pallas_call(
        body,
        in_specs=[pl.BlockSpec(memory_space=space) for space in spaces],
        out_specs=[pl.BlockSpec(memory_space=pltpu.VMEM)] * len(shapes),
        out_shape=[jax.ShapeDtypeStruct(*shape) for shape in shapes],
        scratch_shapes=list(scratch),
        compiler_params=pltpu.CompilerParams(vmem_limit_bytes=limit_mib * 2**20),
        cost_estimate=pl.CostEstimate(flops=flops, bytes_accessed=2**20, transcendentals=0),
    )(*scalars, *far, *args)


PARTS = 4


def fetch(source, target, sem):
    copy = pltpu.make_async_copy(source, target, sem)
    copy.start()
    return copy


class Stream:
    def __init__(self, source, target, sems, parts=PARTS, ahead=2):
        size = source.shape[0] // parts
        at = [pl.ds(k * size, size) for k in range(parts)]
        self.copies = [
            pltpu.make_async_copy(source.at[x], target.at[x], sems.at[k])
            for k, x in enumerate(at)
        ]
        self.size = size
        self.started = 0
        self.waited = 0
        self.start(ahead)

    def start(self, count):
        for copy in self.copies[self.started : self.started + count]:
            copy.start()
        self.started = min(len(self.copies), self.started + count)

    def need(self, upto):
        while self.waited * self.size < upto:
            self.copies[self.waited].wait()
            self.waited += 1
            self.start(1)


def three(x):
    top = x.astype(BF16).astype(F32)
    middle = (x - top).astype(BF16).astype(F32)
    return top, middle, x - top - middle


def joined(x, step):
    return x + pltpu.roll(x, LANES - step, 1) + pltpu.roll(x, LANES - 2 * step, 1)


def iota(shape, axis):
    return lax.broadcasted_iota(jnp.int32, shape, axis)


def send_body(me, table_far, ids_far, nope_far, rope_far, *refs, shards, capacity, apart):
    refs = list(refs)
    table, ids, nope, rope, sems = refs[-5:]
    pairs = ((table_far, table), (ids_far, ids), (nope_far, nope), (rope_far, rope))
    copies = [fetch(a, b, sems.at[k]) for k, (a, b) in enumerate(pairs)]
    copies[0].wait()
    copies[1].wait()
    prefixes = table.shape[0]
    requests = ids.shape[1]
    named = ids[...]
    slot = jnp.zeros((1, requests), jnp.int32)
    for p in range(prefixes):
        slot = slot + jnp.where(named == p, table[p], 0)
    hits = (slot == iota((prefixes, requests), 0)).astype(F32)
    before = iota((requests, requests), 0) < iota((requests, requests), 1)
    earlier = jnp.dot(hits, before.astype(F32), preferred_element_type=F32)
    rank = jnp.sum(earlier * hits, axis=0, keepdims=True).astype(jnp.int32)
    groups = prefixes // shards
    rows = groups * capacity
    row = iota((rows, requests), 0)
    width = nope.shape[1]
    copies[2].wait()
    copies[3].wait()
    for w in range(shards):
        owner = row // capacity
        if w in apart:
            owner = owner ^ me[0]
        pick = (slot == owner * shards + w) & (rank == row % capacity)
        sel = pick.astype(F32).astype(BF16)
        filled = jnp.sum(pick.astype(F32), axis=1, keepdims=True)
        parts = (
            (0, jnp.dot(sel, nope[...], preferred_element_type=F32)),
            (width, jnp.dot(sel, rope[...], preferred_element_type=F32)),
            (width + rope.shape[1], jnp.broadcast_to(filled, (rows, LANES))),
        )
        outs = [refs.pop(0) for _ in range(groups if w in apart else 1)]
        each = rows // len(outs)
        for k, out in enumerate(outs):
            for at, part in parts:
                out[:, at : at + part.shape[1]] = part[k * each : (k + 1) * each].astype(BF16)
        refs.pop(0)[...] = sel


def make_send(me, ids, table, q_nope, q_rope, groups, shards, capacity, apart):
    rows = groups * capacity
    requests = q_nope.shape[0]
    width = q_nope.shape[1] + q_rope.shape[1] + LANES
    counts = [groups if w in apart else 1 for w in range(shards)]
    shapes = []
    for count in counts:
        shapes += [((rows // count, width), BF16)] * count + [((rows, requests), BF16)]
    made = call(
        functools.partial(send_body, shards=shards, capacity=capacity, apart=apart),
        shapes,
        8,
        2 * shards * rows * requests * width,
        scratch=[
            pltpu.SMEM(table.shape, jnp.int32),
            pltpu.VMEM((1, requests), jnp.int32),
            pltpu.VMEM(q_nope.shape, BF16),
            pltpu.VMEM(q_rope.shape, BF16),
            pltpu.SemaphoreType.DMA((4,)),
        ],
        scalars=[me],
        far=[table, ids.reshape(1, requests), q_nope, q_rope],
    )
    made = list(made)
    sends, places = [], []
    for count in counts:
        sends.append([made.pop(0) for _ in range(count)])
        places.append(made.pop(0))
    return sends, places


def head_place(step, block, j, heads):
    return (j % 2) * (heads // 2) + step * (block // 2) + j // 2


def latent_body(me, nope_far, rope_far, w_uk_far, *refs, shares):
    outs = refs[: sum(shares)]
    q_all, rope_all, nope, rope, w_uk, sems = refs[sum(shares) :]
    copy_rope = fetch(rope_far, rope, sems.at[PARTS])
    copy_nope = fetch(nope_far, nope, sems.at[PARTS + 1])
    stream = Stream(w_uk_far, w_uk, sems)
    requests = nope.shape[0]
    heads, width, wide = w_uk.shape
    blocks = wide // LANES
    half = heads // 2
    copy_rope.wait()
    for j in range(half):
        rope_all[pl.ds(j, requests, stride=half), :] = rope[
            :, j * LANES : (j + 1) * LANES
        ].astype(F32)
    copy_nope.wait()
    for h in range(heads):
        stream.need(h + 1)
        value = jnp.dot(
            nope[:, h * width : (h + 1) * width], w_uk[h], preferred_element_type=F32
        )
        for b in range(blocks):
            q_all[b, pl.ds(head_place(0, heads, h, heads), requests, stride=heads), :] = value[
                :, b * LANES : (b + 1) * LANES
            ]
    share = requests // len(shares)
    outs = list(outs)
    for s, parts in enumerate(shares):
        there = me[0] ^ s
        each = share // parts
        some = each // blocks
        for piece in range(parts):
            ref = outs.pop(0)
            first = there * share + piece * each
            rows = each * heads
            for b in range(blocks):
                lanes = slice(b * LANES, (b + 1) * LANES)
                base = pl.multiple_of(first * heads, heads)
                ref[0:rows, lanes] = q_all[b, pl.ds(base, rows), :].astype(BF16)
                base = pl.multiple_of((first + b * some) * half, half)
                ref[rows:, lanes] = rope_all[pl.ds(base, some * half), :].astype(BF16)


def latent_queries(me, q_nope, q_rope, w_uk, shares):
    requests = q_nope.shape[0]
    heads, width, wide = w_uk.shape
    share = requests // len(shares)
    shapes = []
    for parts in shares:
        each = share // parts
        rows = each * heads + each * q_rope.shape[1] // wide
        shapes += [((rows, wide), BF16)] * parts
    return call(
        functools.partial(latent_body, shares=shares),
        shapes,
        14,
        4 * requests * heads * width * wide,
        scratch=[
            pltpu.VMEM((wide // LANES, requests * heads, LANES), F32),
            pltpu.VMEM((requests * heads // 2, LANES), F32),
            pltpu.VMEM(q_nope.shape, BF16),
            pltpu.VMEM(q_rope.shape, BF16),
            pltpu.VMEM(w_uk.shape, BF16),
            pltpu.SemaphoreType.DMA((PARTS + 2,)),
        ],
        scalars=[me],
        far=[q_nope, q_rope, w_uk],
    )


TAIL = 16


def suffix_body(me, lengths, cache_far, keys_far, *refs, sources, count, first, scale):
    asks, outs = refs[:sources], refs[sources : 2 * sources]
    cache, keys, lse_all, sems, sems_keys = refs[2 * sources :]
    wide = asks[0].shape[1]
    dims, tokens = keys.shape[1:]
    heads = asks[0].shape[0] * wide // (count * (wide + dims))
    half = heads // 2
    some = count // (wide // LANES)
    mine = pl.ds(first, count)
    unroll = math.gcd(8, count)
    parts = 2 * count // unroll
    stream_keys = Stream(keys_far.at[mine], keys, sems_keys, parts)
    stream = Stream(cache_far.at[mine], cache, sems, parts)
    share = cache_far.shape[0]
    half_lane = iota((half, 2 * dims), 1)
    rows = sources * heads
    position = iota((rows, tokens), 1)
    diag = iota((rows, LANES), 0) == iota((rows, LANES), 1)
    for step in range(count // unroll):
        at = [step * unroll + u for u in range(unroll)]
        scores = []
        for r in at:
            stream_keys.need(r + 1)
            stream.need(r + 1)
            query = jnp.concatenate([q[r * heads : (r + 1) * heads] for q in asks], axis=0)
            pairs = []
            for ref in asks:
                low = count * heads + (r % some) * half
                pair = ref[low : low + half, r // some * LANES : (r // some + 1) * LANES]
                zero = jnp.zeros_like(pair)
                pairs.append(jnp.where(half_lane < dims, pair, zero))
                pairs.append(jnp.where(half_lane < dims, zero, pair))
            rotary = jnp.concatenate(pairs, axis=0)
            key = keys[r]
            both = jnp.concatenate([key, key], axis=0)
            s = lax.dot_general(query, cache[r], NT, preferred_element_type=F32)
            s = s + jnp.dot(rotary, both, preferred_element_type=F32)
            length = lengths[me[0] * share + first + r]
            scores.append(jnp.where(position < length, s, F32(-1e30)))
        highest = [jnp.max(s, axis=1, keepdims=True) for s in scores]
        weights = [jnp.exp2((s - m) * scale) for s, m in zip(scores, highest)]
        summed = [jnp.sum(w, axis=1, keepdims=True) for w in weights]
        for r, w, m, total in zip(at, weights, highest, summed):
            value = jnp.dot(w.astype(BF16), cache[r], preferred_element_type=F32)
            value = (value * (1.0 / total)).astype(BF16)
            for s in range(sources):
                outs[s][r * heads : (r + 1) * heads, :] = value[s * heads : (s + 1) * heads]
            lse = m * scale + jnp.log2(total)
            lse_all[r : r + 1, :] = jnp.sum(
                jnp.where(diag, lse, F32(0.0)), axis=0, keepdims=True
            )
    if count < TAIL:
        lse_all[count:, :] = jnp.zeros((TAIL - count, LANES), F32)
    lane = iota((TAIL, LANES), 1)
    lse = lse_all[...]
    for s in range(sources):
        x = pltpu.roll(lse, (LANES - s * heads) % LANES, 1)
        top, middle, low = three(jnp.where(lane < heads, x, F32(0.0)))
        x = top + pltpu.roll(middle, heads, 1) + pltpu.roll(low, 2 * heads, 1)
        outs[s][count * heads :, 0:LANES] = x.astype(BF16)
        outs[s][count * heads :, LANES:] = jnp.zeros((TAIL, wide - LANES), BF16)


def suffix_attention(me, lengths, asks, cache, keys, heads, count, first, scale):
    sources = len(asks)
    tokens, wide = cache.shape[1:]
    dims = keys.shape[1]
    parts = 2 * count // math.gcd(8, count)
    return call(
        functools.partial(
            suffix_body, sources=sources, count=count, first=first, scale=scale
        ),
        [((count * heads + TAIL, wide), BF16)] * sources,
        12,
        2 * sources * heads * count * tokens * (2 * wide + dims) * 4,
        scratch=[
            pltpu.VMEM((count, tokens, wide), BF16),
            pltpu.VMEM((count, dims, tokens), BF16),
            pltpu.VMEM((TAIL, LANES), F32),
            pltpu.SemaphoreType.DMA((parts,)),
            pltpu.SemaphoreType.DMA((parts,)),
        ],
        scalars=[me, lengths],
        far=[cache, keys],
        args=asks,
    )


def owner_body(w_uk_far, w_uv_far, latent_far, keys_far, *refs, arrays, index, sizes, scale):
    pieces, outs = refs[:arrays], refs[arrays : 2 * arrays]
    received, packed, query, both, result, latent, w_uk, w_uv = refs[2 * arrays : -3]
    sems, sems_uk, sems_uv = refs[-3:]
    slots = received.shape[0]
    heads, width, wide = w_uk.shape
    values = w_uv.shape[2]
    dims, tokens = keys_far.shape[1:]
    base = heads * values
    rope_at = heads * width
    stream_uk = Stream(w_uk_far, w_uk, sems_uk, PARTS, 1)
    copies = [
        fetch(latent_far.at[index], latent, sems.at[0]),
        fetch(keys_far.at[index], both.at[0:dims], sems.at[1]),
        fetch(keys_far.at[index], both.at[dims : 2 * dims], sems.at[2]),
    ]
    each = slots // arrays
    for k, piece in enumerate(pieces):
        received[k * each : (k + 1) * each, :] = piece[...].astype(received.dtype)
    filled = received[:, rope_at + heads * dims : rope_at + heads * dims + 1].astype(F32)
    here, there = iota((slots, slots), 0), iota((slots, slots), 1)
    filled_row = jnp.sum(jnp.where(here == there, filled, F32(0.0)), axis=0, keepdims=True)
    ahead = jnp.sum(jnp.where(here < there, filled, F32(0.0)), axis=0, keepdims=True)
    move = jnp.where((here == ahead.astype(jnp.int32)) & (filled_row > 0.5), 1.0, 0.0)
    move = move.astype(BF16)
    count = jnp.sum(filled_row).astype(jnp.int32)
    packed[...] = jnp.dot(
        move,
        received[:, 0 : rope_at + heads * dims].astype(BF16),
        preferred_element_type=F32,
    ).astype(BF16)
    for copy in copies:
        copy.wait()
    stream_uk.start(PARTS)
    stream_uv = Stream(w_uv_far, w_uv, sems_uv, PARTS, PARTS)
    part = heads // PARTS

    def attend(rows):
        block = min(heads, 512 // rows // 2 * 2)
        while heads % block:
            block -= 2
        lane = iota((rows, 2 * dims), 1)
        column = iota((rows, LANES), 1)
        chunk = 512
        result[0:rows, base:] = jnp.zeros((rows, LANES), BF16)

        def arrive(copies, step):
            if block % part:
                for k in range(PARTS):
                    pl.when(step == 0)(copies[k].wait)
                return
            for k in range(PARTS):
                pl.when(step == k * part // block)(copies[k].wait)

        def some_heads(step, _):
            arrive(stream_uk.copies, step)
            for j in range(block):
                head = step * block + j
                at = slice(j * rows, (j + 1) * rows)
                nope = packed[0:rows, pl.ds(pl.multiple_of(head * width, LANES), width)]
                query[at, 0:wide] = jnp.dot(
                    nope, w_uk[head], preferred_element_type=F32
                ).astype(BF16)
                if j % 2 == 0:
                    pair_at = pl.multiple_of(rope_at + head * dims, LANES)
                    pair = packed[0:rows, pl.ds(pair_at, 2 * dims)]
                keep = (lane < dims) if j % 2 == 0 else (lane >= dims)
                query[at, wide:] = jnp.where(keep, pair, jnp.zeros_like(pair))
            q_latent = query[0 : block * rows, 0:wide]
            q_rotary = query[0 : block * rows, wide:]
            scores = []
            for t in range(0, tokens, chunk):
                s = lax.dot_general(
                    q_latent, latent[t : t + chunk, :], NT, preferred_element_type=F32
                )
                scores.append(
                    s + jnp.dot(q_rotary, both[:, t : t + chunk], preferred_element_type=F32)
                )
            highest = functools.reduce(
                jnp.maximum, [jnp.max(s, axis=1, keepdims=True) for s in scores]
            )
            summed = None
            mixed = None
            for s, t in zip(scores, range(0, tokens, chunk)):
                weights = jnp.exp2((s - highest) * scale)
                part = jnp.sum(weights, axis=1, keepdims=True)
                product = jnp.dot(
                    weights.astype(BF16),
                    latent[t : t + chunk, :],
                    preferred_element_type=F32,
                )
                summed = part if summed is None else summed + part
                mixed = product if mixed is None else mixed + product
            mixed = (mixed * (1.0 / summed)).astype(BF16)
            lse = highest * scale + jnp.log2(summed)
            tail = jnp.zeros((rows, LANES), F32)
            arrive(stream_uv.copies, step)
            for j in range(block):
                at = slice(j * rows, (j + 1) * rows)
                head = step * block + j
                value = jnp.dot(mixed[at], w_uv[head], preferred_element_type=F32)
                result[0:rows, pl.ds(pl.multiple_of(head * values, LANES), values)] = (
                    value.astype(BF16)
                )
                top, middle, low = three(lse[at])
                place = head_place(step, block, j, heads)
                tail = jnp.where(column == place, top, tail)
                tail = jnp.where(column == heads + place, middle, tail)
                tail = jnp.where(column == 2 * heads + place, low, tail)
            result[0:rows, base:] = (result[0:rows, base:].astype(F32) + tail).astype(BF16)
            return 0

        lax.fori_loop(0, heads // block, some_heads, 0)
        answer = lax.dot_general(
            move[0:rows], result[0:rows, :], TN, preferred_element_type=F32
        )
        for k, out in enumerate(outs):
            out[...] = answer[k * each : (k + 1) * each].astype(BF16)

    for low, high in zip((-1,) + sizes[:-1], sizes):
        pl.when((count > low) & (count <= high))(functools.partial(attend, high))


def owner_attention(received, w_uk, w_uv, latent, keys, index, scale):
    arrays = len(received)
    each = received[0].shape[0]
    slots = arrays * each
    heads, width, wide = w_uk.shape
    values = w_uv.shape[2]
    tokens = latent.shape[1]
    dims = keys.shape[1]
    sizes = {-(-(slots * part // 4) // 16) * 16 for part in (2, 3)}
    sizes = tuple(sorted(x for x in sizes if x < slots)) + (slots,)
    return call(
        functools.partial(owner_body, arrays=arrays, index=index, sizes=sizes, scale=scale),
        [((each, heads * values + LANES), BF16)] * arrays,
        34,
        2 * heads * slots * tokens * (2 * wide + dims),
        scratch=[
            pltpu.VMEM((slots, received[0].shape[1]), F32),
            pltpu.VMEM((slots, heads * (width + dims)), BF16),
            pltpu.VMEM((max(512, 2 * slots), wide + 2 * dims), BF16),
            pltpu.VMEM((2 * dims, tokens), BF16),
            pltpu.VMEM((slots, heads * values + LANES), BF16),
            pltpu.VMEM((tokens, wide), BF16),
            pltpu.VMEM(w_uk.shape, BF16),
            pltpu.VMEM(w_uv.shape, BF16),
            pltpu.SemaphoreType.DMA((3,)),
            pltpu.SemaphoreType.DMA((PARTS,)),
            pltpu.SemaphoreType.DMA((PARTS,)),
        ],
        far=[w_uk, w_uv, latent, keys],
        args=received,
    )


def project_body(me, w_uv_far, *refs, shares):
    tells = list(refs[: sum(shares)])
    out, lse_out, s_all, w_uv, sems = refs[sum(shares) :]
    stream = Stream(w_uv_far, w_uv, sems)
    heads, wide, values = w_uv.shape
    requests = out.shape[0]
    blocks = wide // LANES
    share = requests // len(shares)
    for s, parts in enumerate(shares):
        there = me[0] ^ s
        each = share // parts
        for piece in range(parts):
            ref = tells.pop(0)
            first = there * share + piece * each
            rows = each * heads
            base = pl.multiple_of(first * heads, heads)
            for b in range(blocks):
                part = ref[0:rows, b * LANES : (b + 1) * LANES].astype(F32)
                s_all[b, pl.ds(base, rows), :] = part
            lse = joined(ref[rows:, 0:LANES].astype(F32), heads)
            lse_out[pl.ds(pl.multiple_of(first, each), each), :] = lse[0:each]
    for h in range(heads):
        stream.need(h + 1)
        place = head_place(0, heads, h, heads)
        rows = [
            s_all[b, pl.ds(place, requests, stride=heads), :].astype(BF16) for b in range(blocks)
        ]
        value = jnp.dot(jnp.concatenate(rows, axis=1), w_uv[h], preferred_element_type=F32)
        out[:, h * values : (h + 1) * values] = value.astype(BF16)


def project(me, tells, w_uv, requests, shares):
    heads, wide, values = w_uv.shape
    return call(
        functools.partial(project_body, shares=shares),
        [((requests, heads * values), BF16), ((requests, LANES), F32)],
        14,
        4 * requests * heads * wide * values,
        scratch=[
            pltpu.VMEM((wide // LANES, requests * heads, LANES), F32),
            pltpu.VMEM(w_uv.shape, BF16),
            pltpu.SemaphoreType.DMA((PARTS,)),
        ],
        scalars=[me],
        far=[w_uv],
        args=tells,
    )


def mix_body(*refs, arrays, heads):
    refs = list(refs)
    places = [refs.pop(0) for _ in arrays]
    backs = [[refs.pop(0) for _ in range(n)] for n in arrays]
    suffix, lse_s, out = refs[:3]
    scratches = refs[3:]
    values = out.shape[1] // heads
    for parts, scratch in zip(backs, scratches):
        each = parts[0].shape[0]
        for k, part in enumerate(parts):
            scratch[k * each : (k + 1) * each, :] = part[...].astype(F32)

    def gather(lo, hi):
        found = [
            lax.dot_general(p[...], b[:, lo:hi].astype(BF16), TN, preferred_element_type=F32)
            for p, b in zip(places, scratches)
        ]
        return functools.reduce(jnp.add, found)

    lse_p = joined(gather(heads * values, heads * values + LANES), heads)
    lse_s = lse_s[...]
    overall = jnp.maximum(lse_p, lse_s)
    a = jnp.exp2(lse_p - overall)
    b = jnp.exp2(lse_s - overall)
    total = 1.0 / (a + b)
    a = a * total
    b = b * total
    some = 4
    for first in range(0, heads, some):
        prefix = gather(first * values, (first + some) * values)
        for h in range(first, first + some):
            place = head_place(0, heads, h, heads)
            at = slice(h * values, (h + 1) * values)
            mine = prefix[:, (h - first) * values : (h - first + 1) * values]
            mixed = (
                a[:, place : place + 1] * mine
                + b[:, place : place + 1] * suffix[:, at].astype(F32)
            )
            out[:, at] = mixed.astype(BF16)


def mix(places, backs, suffix, lse, heads):
    requests, width = suffix.shape
    arrays = tuple(len(parts) for parts in backs)
    rows = places[0].shape[0]
    return call(
        functools.partial(mix_body, arrays=arrays, heads=heads),
        [((requests, width), BF16)],
        8,
        2 * requests * rows * width,
        scratch=[pltpu.VMEM((rows, width + LANES), F32)] * len(arrays),
        args=[*places, *[x for parts in backs for x in parts], suffix, lse],
    )[0]


def local(
    q_nope,
    q_rope,
    w_uk,
    w_uv,
    prefix_latent,
    prefix_rope,
    suffix_latent,
    suffix_rope,
    suffix_len,
    request_prefix,
    prefix_slot,
):
    groups = lax.axis_size("grp")
    ranks = lax.axis_size("tp")
    requests = q_nope.shape[0]
    prefixes = prefix_slot.shape[0]
    shards = prefix_latent.shape[0]
    capacity = max(2, 2 * requests // prefixes)
    scale = math.log2(math.e) / math.sqrt(w_uk.shape[1] + prefix_rope.shape[1])
    share = requests // ranks
    heads = w_uk.shape[0]
    near, pieces = min(2, ranks), 2
    shares = (1,) * near + (pieces,) * (ranks - near)
    apart = (shards - 1,)
    mine = lax.axis_index("grp").astype(jnp.int32).reshape(1)
    me = lax.axis_index("tp").astype(jnp.int32).reshape(1)
    lengths = suffix_len.reshape(-1)

    def swap(x, s, axis, size):
        if s == 0:
            return x
        return lax.ppermute(x, axis, [(k, k ^ s) for k in range(size)])

    def exchange(xs):
        if len(xs) > 1:
            return [swap(x, s, "grp", groups) for s, x in enumerate(xs)]
        return [lax.all_to_all(xs[0], "grp", split_axis=0, concat_axis=0, tiled=True)]

    sends, places = make_send(
        mine, request_prefix, prefix_slot, q_nope, q_rope, groups, shards, capacity, apart
    )
    received = [exchange(x) for x in sends]

    made = list(latent_queries(me, q_nope, q_rope, w_uk, shares))
    asks = [
        [swap(made.pop(0), s, "tp", ranks) for _ in range(parts)]
        for s, parts in enumerate(shares)
    ]

    def attend(some, p, count):
        return suffix_attention(
            me,
            lengths,
            [asks[s][p] for s in some],
            suffix_latent,
            suffix_rope,
            heads,
            count,
            p * count,
            scale,
        )

    tells = [[None] * parts for parts in shares]
    for s, x in enumerate(attend(range(near), 0, share)):
        tells[s][0] = swap(x, s, "tp", ranks)
    for p in range(pieces):
        for s, x in enumerate(attend(range(near, ranks), p, share // pieces), near):
            tells[s][p] = swap(x, s, "tp", ranks)

    backs = []
    for w in range(shards):
        result = owner_attention(
            received[w], w_uk, w_uv, prefix_latent, prefix_rope, w, scale
        )
        backs.append(exchange(result))
    suffix, lse = project(me, [x for parts in tells for x in parts], w_uv, requests, shares)
    return mix(places, backs, suffix, lse, heads)


def solution(mesh):
    in_specs = (
        P("grp", "tp"),
        P("grp", "tp"),
        P("tp", None, None),
        P("tp", None, None),
        P("grp", None, None),
        P("grp", None, None),
        P(("grp", "tp"), None, None),
        P(("grp", "tp"), None, None),
        P("grp", None),
        P("grp"),
        P(),
    )

    return jax.shard_map(
        local, mesh=mesh, in_specs=in_specs, out_specs=P("grp", "tp"), check_vma=False
    )
```

profile of v0, /device:TPU:0, one launch (start us, length us, event | category | flops | bytes accessed | tf_op | source)
XLA Modules:
  0.0 120.2 jit_solution(14216569496590971561)
XLA Ops:
  0.0 2.7 %shard_map.109 = (bf16[64,6272]{1,0:T(8,128)(2,1)}, bf16[64,64]{1,0:T(8,128)(2,1)S(1)}, bf16[8,6272]{1,0:T(8,128)(2,1)S(1)}, bf16[8,6272]{1,0:T(8,128)(2,1)}, bf...) custom-call(s32[1]{0:T(128)} %bitcast.me, ...), custom_call_target="tpu_custom_call" | custom-call | flops 102760448 | bytes 1048576 | tf_op jit(solution)/shard_map/pallas_call | solution.py:22
  2.7 7.3 %all-to-all-start = ((bf16[8,8,6272]{2,1,0:T(8,128)(2,1)}), bf16[8,8,6272]{2,1,0:T(8,128)(2,1)S(1)}, u32[]{:S(2)}, u32[]{:S(2)}) async-start(bf16[8,8,6272]{2,1,0:T(8,128)(2,1)} %bitcast.2), calls=%async_computation | async-start | bytes 1605632 | tf_op jit(solution)/shard_map/all_to_all | solution.py:617
  10.0 6.8 %shard_map.112 = (bf16[576,512]{1,0:T(8,128)(2,1)S(1)}, bf16[576,512]{1,0:T(8,128)(2,1)S(1)}, bf16[288,512]{1,0:T(8,128)(2,1)S(1)}, bf16[288,512]{1,0:T(8,128)(2...) custom-call(s32[1]{0:T(128)} %bitcast.6.me, bf16[64,4096]{1,0:T(8,128)(2,1)} %nope_far.3, ...), custom_call_target="tpu_custom_call" | custom-call | flops 536870912 | bytes 1048576 | tf_op jit(solution)/shard_map/pallas_call | solution.py:22
  18.2 2.0 %collective-permute-start = (bf16[8,6272]{1,0:T(8,128)(2,1)}, bf16[8,6272]{1,0:T(8,128)(2,1)S(1)}, u32[]{:S(2)}, u32[]{:S(2)}) collective-permute-start(bf16[8,6272]{1,0:T(8,128)(2,1)} %get-tuple-element.42), channel_id=1, source_target_pairs={{0,4},{4,0},{8,12},{12,8},{16,20},{20,16},{24,28},{28,24},{1,5},{5... | collective-permute-start | bytes 301064 | tf_op jit(solution)/shard_map/ppermute | solution.py:612
  20.2 1.5 %collective-permute-start.1 = (bf16[8,6272]{1,0:T(8,128)(2,1)}, bf16[8,6272]{1,0:T(8,128)(2,1)S(1)}, u32[]{:S(2)}, u32[]{:S(2)}) collective-permute-start(bf16[8,6272]{1,0:T(8,128)(2,1)} %get-tuple-element.43), channel_id=1, source_target_pairs={{0,8},{4,12},{8,0},{12,4},{16,24},{20,28},{24,16},{28,20},{1,9},{5... | collective-permute-start | bytes 301064 | tf_op jit(solution)/shard_map/ppermute | solution.py:612
  21.7 2.9 %collective-permute-start.3 = (bf16[8,6272]{1,0:T(8,128)(2,1)}, bf16[8,6272]{1,0:T(8,128)(2,1)}, u32[]{:S(2)}, u32[]{:S(2)}) collective-permute-start(bf16[8,6272]{1,0:T(8,128)(2,1)} %get-tuple-element.45), channel_id=1, source_target_pairs={{0,16},{4,20},{8,24},{12,28},{16,0},{20,4},{24,8},{28,12},{1,17},{... | collective-permute-start | bytes 301064 | tf_op jit(solution)/shard_map/ppermute | solution.py:612
  26.1 4.7 %shard_map.113 = (bf16[528,512]{1,0:T(8,128)(2,1)S(1)}, bf16[528,512]{1,0:T(8,128)(2,1)S(1)}) custom-call(s32[1]{0:T(128)} %bitcast.6.me, s32[64]{0:T(128)S(1)} %bitcast.10, bf16[16,256,512]{2,1,0:T(8,128)(2,1)} %cache_far.5, bf16[16,64,256]{2,1,0:T(8,128)(2,1)} %keys_far.9, bf16[576,512]{1,0:T(8,128)(2,1)S(1)} %get-tuple-element.57.refs_0_, ...), custom_call_target="tpu_custom_call" | custom-call | flops 2281701376 | bytes 1048576 | tf_op jit(solution)/shard_map/pallas_call | solution.py:22
  31.5 3.3 %collective-permute-start.5 = (bf16[8,6272]{1,0:T(8,128)(2,1)S(1)}, bf16[8,6272]{1,0:T(8,128)(2,1)}, u32[]{:S(2)}, u32[]{:S(2)}) collective-permute-start(bf16[8,6272]{1,0:T(8,128)(2,1)S(1)} %get-tuple-element.47), channel_id=1, source_target_pairs={{0,24},{4,28},{8,16},{12,20},{16,8},{20,12},{24,0},{28,4},{1,25},{... | collective-permute-start | bytes 301064 | tf_op jit(solution)/shard_map/ppermute | solution.py:612
  35.4 3.0 %all-to-all-done = bf16[8,8,6272]{2,1,0:T(8,128)(2,1)S(1)} async-done(((bf16[8,8,6272]{2,1,0:T(8,128)(2,1)}), bf16[8,8,6272]{2,1,0:T(8,128)(2,1)S(1)}, u32[]{:S(2)}, u32[]{:S(2)}) %all-to-all-start) | async-done | bytes 802848 | tf_op jit(solution)/shard_map/all_to_all | solution.py:617
  38.4 13.0 %shard_map.110 = bf16[64,4224]{1,0:T(8,128)(2,1)} custom-call(bf16[32,128,512]{2,1,0:T(8,128)(2,1)} %w_uk_far.5, bf16[32,512,128]{2,1,0:T(8,128)(2,1)} %w_uv_far.5, bf16[2,2048,512]{2,1,0:T(8,128)(2,1)} %latent_far.3, bf16[2,64,2048]{2,1,0:T(8,128)(2,1)} %keys_far.6, bf16[64,6272]{1,0:T(8,128)(2,1)S(1)} %bitcast.9), custom_call_target="tpu_custom_call" | custom-call | flops 9126805504 | bytes 1048576 | tf_op jit(solution)/shard_map/pallas_call | solution.py:22
  51.4 3.5 %all-to-all-start.1 = ((bf16[8,8,4224]{2,1,0:T(8,128)(2,1)}), bf16[8,8,4224]{2,1,0:T(8,128)(2,1)S(1)}, u32[]{:S(2)}, u32[]{:S(2)}) async-start(bf16[8,8,4224]{2,1,0:T(8,128)(2,1)} %bitcast.4), calls=%async_computation.1 | async-start | bytes 1081344 | tf_op jit(solution)/shard_map/all_to_all | solution.py:617
  55.0 1.6 %collective-permute-start.16 = (bf16[288,512]{1,0:T(8,128)(2,1)S(1)}, bf16[288,512]{1,0:T(8,128)(2,1)S(1)}, u32[]{:S(2)}, u32[]{:S(2)}) collective-permute-start(bf16[288,512]{1,0:T(8,128)(2,1)S(1)} %copy-done.4), channel_id=1, source_target_pairs={{0,2},{1,3},{2,0},{3,1},{4,6},{5,7},{6,4},{7,5},{8,10},{9,11},{10,... | collective-permute-start | bytes 884744 | tf_op jit(solution)/shard_map/ppermute | solution.py:612
  60.6 13.4 %shard_map.111 = (bf16[8,4224]{1,0:T(8,128)(2,1)S(1)}, bf16[8,4224]{1,0:T(8,128)(2,1)S(1)}, bf16[8,4224]{1,0:T(8,128)(2,1)S(1)}, bf16[8,4224]{1,0:T(8,128)(2,1)S...) custom-call(bf16[32,128,512]{2,1,0:T(8,128)(2,1)} %w_uk_far.5, ...), custom_call_target="tpu_custom_call" | custom-call | flops 9126805504 | bytes 1048576 | tf_op jit(solution)/shard_map/pallas_call | solution.py:22
  74.0 2.9 %collective-permute-start.10 = (bf16[8,4224]{1,0:T(8,128)(2,1)S(1)}, bf16[8,4224]{1,0:T(8,128)(2,1)S(1)}, u32[]{:S(2)}, u32[]{:S(2)}) collective-permute-start(bf16[8,4224]{1,0:T(8,128)(2,1)S(1)} %get-tuple-element.53), channel_id=1, source_target_pairs={{0,16},{4,20},{8,24},{12,28},{16,0},{20,4},{24,8},{28,12},{1,17},{... | collective-permute-start | bytes 202760 | tf_op jit(solution)/shard_map/ppermute | solution.py:612
  76.9 7.0 %collective-permute-start.11 = (bf16[8,4224]{1,0:T(8,128)(2,1)S(1)}, bf16[8,4224]{1,0:T(8,128)(2,1)S(1)}, u32[]{:S(2)}, u32[]{:S(2)}) collective-permute-start(bf16[8,4224]{1,0:T(8,128)(2,1)S(1)} %get-tuple-element.54), channel_id=1, source_target_pairs={{0,20},{4,16},{8,28},{12,24},{16,4},{20,0},{24,12},{28,8},{1,21},{... | collective-permute-start | bytes 202760 | tf_op jit(solution)/shard_map/ppermute | solution.py:612
  83.9 3.3 %shard_map.114 = (bf16[272,512]{1,0:T(8,128)(2,1)S(1)}, bf16[272,512]{1,0:T(8,128)(2,1)S(1)}) custom-call(s32[1]{0:T(128)} %bitcast.6.me, s32[64]{0:T(128)S(1)} %bitcast.11, bf16[16,256,512]{2,1,0:T(8,128)(2,1)} %cache_far.5, bf16[16,64,256]{2,1,0:T(8,128)(2,1)} %keys_far.9, bf16[288,512]{1,0:T(8,128)(2,1)S(1)} %collective-permute-done.16.refs_0_, ...), custom_call_target="tpu_custom_call" | custom-call | flops 1140850688 | bytes 1048576 | tf_op jit(solution)/shard_map/pallas_call | solution.py:22
  88.6 3.3 %shard_map.115 = (bf16[272,512]{1,0:T(8,128)(2,1)S(1)}, bf16[272,512]{1,0:T(8,128)(2,1)S(1)}) custom-call(s32[1]{0:T(128)} %bitcast.6.me, s32[64]{0:T(128)S(1)} %bitcast.12, bf16[16,256,512]{2,1,0:T(8,128)(2,1)} %cache_far.5, bf16[16,64,256]{2,1,0:T(8,128)(2,1)} %keys_far.9, bf16[288,512]{1,0:T(8,128)(2,1)S(1)} %collective-permute-done.19.refs_0_, ...), custom_call_target="tpu_custom_call" | custom-call | flops 1140850688 | bytes 1048576 | tf_op jit(solution)/shard_map/pallas_call | solution.py:22
  93.0 1.5 %collective-permute-start.23 = (bf16[272,512]{1,0:T(8,128)(2,1)S(1)}, bf16[272,512]{1,0:T(8,128)(2,1)S(1)}, u32[]{:S(2)}, u32[]{:S(2)}) collective-permute-start(bf16[272,512]{1,0:T(8,128)(2,1)S(1)} %get-tuple-element.68), channel_id=1, source_target_pairs={{0,3},{1,2},{2,1},{3,0},{4,7},{5,6},{6,5},{7,4},{8,11},{9,10},{10,... | collective-permute-start | bytes 835592 | tf_op jit(solution)/shard_map/ppermute | solution.py:612
  94.4 2.4 %collective-permute-done.18.refs_2_ = bf16[272,512]{1,0:T(8,128)(2,1)S(1)} collective-permute-done((bf16[272,512]{1,0:T(8,128)(2,1)S(1)}, bf16[272,512]{1,0:T(8,128)(2,1)S(1)}, u32[]{:S(2)}, u32[]{:S(2)}) %collective-permute-start.18) | collective-permute-done | bytes 278560 | tf_op jit(solution)/shard_map/ppermute | solution.py:612
  96.8 6.0 %collective-permute-done.21.refs_3_ = bf16[272,512]{1,0:T(8,128)(2,1)S(1)} collective-permute-done((bf16[272,512]{1,0:T(8,128)(2,1)S(1)}, bf16[272,512]{1,0:T(8,128)(2,1)S(1)}, u32[]{:S(2)}, u32[]{:S(2)}) %collective-permute-start.21) | collective-permute-done | bytes 278560 | tf_op jit(solution)/shard_map/ppermute | solution.py:612
  102.8 4.8 %collective-permute-done.22.refs_4_ = bf16[272,512]{1,0:T(8,128)(2,1)S(1)} collective-permute-done((bf16[272,512]{1,0:T(8,128)(2,1)S(1)}, bf16[272,512]{1,0:T(8,128)(2,1)S(1)}, u32[]{:S(2)}, u32[]{:S(2)}) %collective-permute-start.22) | collective-permute-done | bytes 278560 | tf_op jit(solution)/shard_map/ppermute | solution.py:612
  107.5 4.9 %collective-permute-done.23.refs_5_ = bf16[272,512]{1,0:T(8,128)(2,1)S(1)} collective-permute-done((bf16[272,512]{1,0:T(8,128)(2,1)S(1)}, bf16[272,512]{1,0:T(8,128)(2,1)S(1)}, u32[]{:S(2)}, u32[]{:S(2)}) %collective-permute-start.23) | collective-permute-done | bytes 278560 | tf_op jit(solution)/shard_map/ppermute | solution.py:612
  112.5 5.8 %shard_map.116 = (bf16[64,4096]{1,0:T(8,128)(2,1)S(1)}, f32[64,128]{1,0:T(8,128)S(1)}) custom-call(s32[1]{0:T(128)} %bitcast.6.me, bf16[32,512,128]{2,1,0:T(8,128)(2,1)} %w_uv_far.5, bf16[528,512]{1,0:T(8,128)(2,1)S(1)} %get-tuple-element.59.refs_0_, bf16[528,512]{1,0:T(8,128)(2,1)S(1)} %collective-permute-done.15.refs_1_, ...), custom_call_target="tpu_custom_call" | custom-call | flops 536870912 | bytes 1048576 | tf_op jit(solution)/shard_map/pallas_call | solution.py:22
  118.4 1.7 %shard_map.117 = bf16[64,4096]{1,0:T(8,128)(2,1)} custom-call(bf16[64,64]{1,0:T(8,128)(2,1)S(1)} %get-tuple-element.38.refs_0_, bf16[64,64]{1,0:T(8,128)(2,1)S(1)} %get-tuple-element.39.refs_1_, bf16[64,4224]{1,0:T(8,128)(2,1)S(1)} %bitcast.8, bf16[8,4224]{1,0:T(8,128)(2,1)S(1)} %get-tuple-element.49.refs_3_, ...), custom_call_target="tpu_custom_call" | custom-call | flops 33554432 | bytes 1048576 | tf_op jit(solution)/shard_map/pallas_call | solution.py:22
  (55 shorter events, 10.7 us)
Async XLA Ops:
  2.7 35.7 %all-to-all-start = ((bf16[8,8,6272]{2,1,0:T(8,128)(2,1)}), bf16[8,8,6272]{2,1,0:T(8,128)(2,1)S(1)}, u32[]{:S(2)}, u32[]{:S(2)}) async-start(bf16[8,8,6272]{2,1,0:T(8,128)(2,1)} %bitcast.2), calls=%async_computation | async-start | bytes 1605632 | tf_op jit(solution)/shard_map/all_to_all | solution.py:617
  18.2 6.4 %collective-permute-start.14 = (bf16[576,512]{1,0:T(8,128)(2,1)S(1)}, bf16[576,512]{1,0:T(8,128)(2,1)S(1)}, u32[]{:S(2)}, u32[]{:S(2)}) collective-permute-start(bf16[576,512]{1,0:T(8,128)(2,1)S(1)} %get-tuple-element.58), channel_id=1, source_target_pairs={{0,1},{1,0},{2,3},{3,2},{4,5},{5,4},{6,7},{7,6},{8,9},{9,8},{10,11... | collective-permute-start | bytes 1769480 | tf_op jit(solution)/shard_map/ppermute | solution.py:612
  18.2 12.6 %collective-permute-start = (bf16[8,6272]{1,0:T(8,128)(2,1)}, bf16[8,6272]{1,0:T(8,128)(2,1)S(1)}, u32[]{:S(2)}, u32[]{:S(2)}) collective-permute-start(bf16[8,6272]{1,0:T(8,128)(2,1)} %get-tuple-element.42), channel_id=1, source_target_pairs={{0,4},{4,0},{8,12},{12,8},{16,20},{20,16},{24,28},{28,24},{1,5},{5... | collective-permute-start | bytes 301064 | tf_op jit(solution)/shard_map/ppermute | solution.py:612
  20.2 14.5 %collective-permute-start.1 = (bf16[8,6272]{1,0:T(8,128)(2,1)}, bf16[8,6272]{1,0:T(8,128)(2,1)S(1)}, u32[]{:S(2)}, u32[]{:S(2)}) collective-permute-start(bf16[8,6272]{1,0:T(8,128)(2,1)} %get-tuple-element.43), channel_id=1, source_target_pairs={{0,8},{4,12},{8,0},{12,4},{16,24},{20,28},{24,16},{28,20},{1,9},{5... | collective-permute-start | bytes 301064 | tf_op jit(solution)/shard_map/ppermute | solution.py:612
  21.7 33.2 %collective-permute-start.2 = (bf16[8,6272]{1,0:T(8,128)(2,1)}, bf16[8,6272]{1,0:T(8,128)(2,1)}, u32[]{:S(2)}, u32[]{:S(2)}) collective-permute-start(bf16[8,6272]{1,0:T(8,128)(2,1)} %get-tuple-element.44), channel_id=1, source_target_pairs={{0,12},{4,8},{8,4},{12,0},{16,28},{20,24},{24,20},{28,16},{1,13},{... | collective-permute-start | bytes 301064 | tf_op jit(solution)/shard_map/ppermute | solution.py:612
  21.7 34.8 %collective-permute-start.3 = (bf16[8,6272]{1,0:T(8,128)(2,1)}, bf16[8,6272]{1,0:T(8,128)(2,1)}, u32[]{:S(2)}, u32[]{:S(2)}) collective-permute-start(bf16[8,6272]{1,0:T(8,128)(2,1)} %get-tuple-element.45), channel_id=1, source_target_pairs={{0,16},{4,20},{8,24},{12,28},{16,0},{20,4},{24,8},{28,12},{1,17},{... | collective-permute-start | bytes 301064 | tf_op jit(solution)/shard_map/ppermute | solution.py:612
  24.6 31.9 %collective-permute-start.4 = (bf16[8,6272]{1,0:T(8,128)(2,1)}, bf16[8,6272]{1,0:T(8,128)(2,1)}, u32[]{:S(2)}, u32[]{:S(2)}) collective-permute-start(bf16[8,6272]{1,0:T(8,128)(2,1)} %get-tuple-element.46), channel_id=1, source_target_pairs={{0,20},{4,16},{8,28},{12,24},{16,4},{20,0},{24,12},{28,8},{1,21},{... | collective-permute-start | bytes 301064 | tf_op jit(solution)/shard_map/ppermute | solution.py:612
  31.5 25.6 %collective-permute-start.5 = (bf16[8,6272]{1,0:T(8,128)(2,1)S(1)}, bf16[8,6272]{1,0:T(8,128)(2,1)}, u32[]{:S(2)}, u32[]{:S(2)}) collective-permute-start(bf16[8,6272]{1,0:T(8,128)(2,1)S(1)} %get-tuple-element.47), channel_id=1, source_target_pairs={{0,24},{4,28},{8,16},{12,20},{16,8},{20,12},{24,0},{28,4},{1,25},{... | collective-permute-start | bytes 301064 | tf_op jit(solution)/shard_map/ppermute | solution.py:612
  35.4 23.1 %collective-permute-start.6 = (bf16[8,6272]{1,0:T(8,128)(2,1)S(1)}, bf16[8,6272]{1,0:T(8,128)(2,1)}, u32[]{:S(2)}, u32[]{:S(2)}) collective-permute-start(bf16[8,6272]{1,0:T(8,128)(2,1)S(1)} %get-tuple-element.48), channel_id=1, source_target_pairs={{0,28},{4,24},{8,20},{12,16},{16,12},{20,8},{24,4},{28,0},{1,29},{... | collective-permute-start | bytes 301064 | tf_op jit(solution)/shard_map/ppermute | solution.py:612
  51.4 67.0 %all-to-all-start.1 = ((bf16[8,8,4224]{2,1,0:T(8,128)(2,1)}), bf16[8,8,4224]{2,1,0:T(8,128)(2,1)S(1)}, u32[]{:S(2)}, u32[]{:S(2)}) async-start(bf16[8,8,4224]{2,1,0:T(8,128)(2,1)} %bitcast.4), calls=%async_computation.1 | async-start | bytes 1081344 | tf_op jit(solution)/shard_map/all_to_all | solution.py:617
  55.0 19.0 %collective-permute-start.16 = (bf16[288,512]{1,0:T(8,128)(2,1)S(1)}, bf16[288,512]{1,0:T(8,128)(2,1)S(1)}, u32[]{:S(2)}, u32[]{:S(2)}) collective-permute-start(bf16[288,512]{1,0:T(8,128)(2,1)S(1)} %copy-done.4), channel_id=1, source_target_pairs={{0,2},{1,3},{2,0},{3,1},{4,6},{5,7},{6,4},{7,5},{8,10},{9,11},{10,... | collective-permute-start | bytes 884744 | tf_op jit(solution)/shard_map/ppermute | solution.py:612
  56.6 20.3 %collective-permute-start.17 = (bf16[288,512]{1,0:T(8,128)(2,1)S(1)}, bf16[288,512]{1,0:T(8,128)(2,1)S(1)}, u32[]{:S(2)}, u32[]{:S(2)}) collective-permute-start(bf16[288,512]{1,0:T(8,128)(2,1)S(1)} %copy-done.2), channel_id=1, source_target_pairs={{0,3},{1,2},{2,1},{3,0},{4,7},{5,6},{6,5},{7,4},{8,11},{9,10},{10,... | collective-permute-start | bytes 884744 | tf_op jit(solution)/shard_map/ppermute | solution.py:612
  56.6 30.6 %collective-permute-start.19 = (bf16[288,512]{1,0:T(8,128)(2,1)S(1)}, bf16[288,512]{1,0:T(8,128)(2,1)S(1)}, u32[]{:S(2)}, u32[]{:S(2)}) collective-permute-start(bf16[288,512]{1,0:T(8,128)(2,1)S(1)} %get-tuple-element.64), channel_id=1, source_target_pairs={{0,2},{1,3},{2,0},{3,1},{4,6},{5,7},{6,4},{7,5},{8,10},{9,11},{10,... | collective-permute-start | bytes 884744 | tf_op jit(solution)/shard_map/ppermute | solution.py:612
  57.2 31.4 %collective-permute-start.20 = (bf16[288,512]{1,0:T(8,128)(2,1)S(1)}, bf16[288,512]{1,0:T(8,128)(2,1)S(1)}, u32[]{:S(2)}, u32[]{:S(2)}) collective-permute-start(bf16[288,512]{1,0:T(8,128)(2,1)S(1)} %get-tuple-element.65), channel_id=1, source_target_pairs={{0,3},{1,2},{2,1},{3,0},{4,7},{5,6},{6,5},{7,4},{8,11},{9,10},{10,... | collective-permute-start | bytes 884744 | tf_op jit(solution)/shard_map/ppermute | solution.py:612
  58.6 53.9 %collective-permute-start.15 = (bf16[528,512]{1,0:T(8,128)(2,1)S(1)}, bf16[528,512]{1,0:T(8,128)(2,1)S(1)}, u32[]{:S(2)}, u32[]{:S(2)}) collective-permute-start(bf16[528,512]{1,0:T(8,128)(2,1)S(1)} %get-tuple-element.60), channel_id=1, source_target_pairs={{0,1},{1,0},{2,3},{3,2},{4,5},{5,4},{6,7},{7,6},{8,9},{9,8},{10,11... | collective-permute-start | bytes 1622024 | tf_op jit(solution)/shard_map/ppermute | solution.py:612
  74.0 18.7 %collective-permute-start.10 = (bf16[8,4224]{1,0:T(8,128)(2,1)S(1)}, bf16[8,4224]{1,0:T(8,128)(2,1)S(1)}, u32[]{:S(2)}, u32[]{:S(2)}) collective-permute-start(bf16[8,4224]{1,0:T(8,128)(2,1)S(1)} %get-tuple-element.53), channel_id=1, source_target_pairs={{0,16},{4,20},{8,24},{12,28},{16,0},{20,4},{24,8},{28,12},{1,17},{... | collective-permute-start | bytes 202760 | tf_op jit(solution)/shard_map/ppermute | solution.py:612
  76.9 16.1 %collective-permute-start.11 = (bf16[8,4224]{1,0:T(8,128)(2,1)S(1)}, bf16[8,4224]{1,0:T(8,128)(2,1)S(1)}, u32[]{:S(2)}, u32[]{:S(2)}) collective-permute-start(bf16[8,4224]{1,0:T(8,128)(2,1)S(1)} %get-tuple-element.54), channel_id=1, source_target_pairs={{0,20},{4,16},{8,28},{12,24},{16,4},{20,0},{24,12},{28,8},{1,21},{... | collective-permute-start | bytes 202760 | tf_op jit(solution)/shard_map/ppermute | solution.py:612
  87.2 9.6 %collective-permute-start.18 = (bf16[272,512]{1,0:T(8,128)(2,1)S(1)}, bf16[272,512]{1,0:T(8,128)(2,1)S(1)}, u32[]{:S(2)}, u32[]{:S(2)}) collective-permute-start(bf16[272,512]{1,0:T(8,128)(2,1)S(1)} %get-tuple-element.63), channel_id=1, source_target_pairs={{0,2},{1,3},{2,0},{3,1},{4,6},{5,7},{6,4},{7,5},{8,10},{9,11},{10,... | collective-permute-start | bytes 835592 | tf_op jit(solution)/shard_map/ppermute | solution.py:612
  91.9 10.9 %collective-permute-start.21 = (bf16[272,512]{1,0:T(8,128)(2,1)S(1)}, bf16[272,512]{1,0:T(8,128)(2,1)S(1)}, u32[]{:S(2)}, u32[]{:S(2)}) collective-permute-start(bf16[272,512]{1,0:T(8,128)(2,1)S(1)} %get-tuple-element.66), channel_id=1, source_target_pairs={{0,2},{1,3},{2,0},{3,1},{4,6},{5,7},{6,4},{7,5},{8,10},{9,11},{10,... | collective-permute-start | bytes 835592 | tf_op jit(solution)/shard_map/ppermute | solution.py:612
  92.7 14.8 %collective-permute-start.22 = (bf16[272,512]{1,0:T(8,128)(2,1)S(1)}, bf16[272,512]{1,0:T(8,128)(2,1)S(1)}, u32[]{:S(2)}, u32[]{:S(2)}) collective-permute-start(bf16[272,512]{1,0:T(8,128)(2,1)S(1)} %get-tuple-element.67), channel_id=1, source_target_pairs={{0,3},{1,2},{2,1},{3,0},{4,7},{5,6},{6,5},{7,4},{8,11},{9,10},{10,... | collective-permute-start | bytes 835592 | tf_op jit(solution)/shard_map/ppermute | solution.py:612
  93.0 19.5 %collective-permute-start.23 = (bf16[272,512]{1,0:T(8,128)(2,1)S(1)}, bf16[272,512]{1,0:T(8,128)(2,1)S(1)}, u32[]{:S(2)}, u32[]{:S(2)}) collective-permute-start(bf16[272,512]{1,0:T(8,128)(2,1)S(1)} %get-tuple-element.68), channel_id=1, source_target_pairs={{0,3},{1,2},{2,1},{3,0},{4,7},{5,6},{6,5},{7,4},{8,11},{9,10},{10,... | collective-permute-start | bytes 835592 | tf_op jit(solution)/shard_map/ppermute | solution.py:612
  96.8 21.6 %collective-permute-start.12 = (bf16[8,4224]{1,0:T(8,128)(2,1)S(1)}, bf16[8,4224]{1,0:T(8,128)(2,1)S(1)}, u32[]{:S(2)}, u32[]{:S(2)}) collective-permute-start(bf16[8,4224]{1,0:T(8,128)(2,1)S(1)} %get-tuple-element.55), channel_id=1, source_target_pairs={{0,24},{4,28},{8,16},{12,20},{16,8},{20,12},{24,0},{28,4},{1,25},{... | collective-permute-start | bytes 202760 | tf_op jit(solution)/shard_map/ppermute | solution.py:612
  102.8 15.6 %collective-permute-start.13 = (bf16[8,4224]{1,0:T(8,128)(2,1)S(1)}, bf16[8,4224]{1,0:T(8,128)(2,1)S(1)}, u32[]{:S(2)}, u32[]{:S(2)}) collective-permute-start(bf16[8,4224]{1,0:T(8,128)(2,1)S(1)} %get-tuple-element.56), channel_id=1, source_target_pairs={{0,28},{4,24},{8,20},{12,16},{16,12},{20,8},{24,4},{28,0},{1,29},{... | collective-permute-start | bytes 202760 | tf_op jit(solution)/shard_map/ppermute | solution.py:612
  107.5 10.8 %collective-permute-start.7 = (bf16[8,4224]{1,0:T(8,128)(2,1)S(1)}, bf16[8,4224]{1,0:T(8,128)(2,1)S(1)}, u32[]{:S(2)}, u32[]{:S(2)}) collective-permute-start(bf16[8,4224]{1,0:T(8,128)(2,1)S(1)} %get-tuple-element.50), channel_id=1, source_target_pairs={{0,4},{4,0},{8,12},{12,8},{16,20},{20,16},{24,28},{28,24},{1,5},{5... | collective-permute-start | bytes 202760 | tf_op jit(solution)/shard_map/ppermute | solution.py:612
  (11 other events, 77.2 us)
where the time goes:
time: 122 us; the launch traced here: 120 us
  Pallas kernels  54.8 us (45%)
  starting transfers between devices  39.6 us (32%)
  waiting for transfers between devices  21.1 us (17%)
  local copies, waits for them, and re-layouts  4.48 us (4%)
    pallas_call x9, Pallas kernels, call(): pl.pallas_call(body, in_specs=[pl.BlockSpec(memory_space=space) for space...  54.8 us
    ppermute x24, starting transfers between devices, swap(): return lax.ppermute(x, axis, [(k, k ^ s) for k in range(size)])  28.7 us
    ppermute x24, waiting for transfers between devices, swap(): return lax.ppermute(x, axis, [(k, k ^ s) for k in range(size)])  18.1 us
    all_to_all x2, starting transfers between devices, exchange(): lax.all_to_all(xs[0], 'grp', split_axis=0, concat_axis=0, tiled=True)  10.8 us
    unnamed x18, local copies, waits for them, and re-layouts  4.48 us
    all_to_all x2, waiting for transfers between devices, exchange(): lax.all_to_all(xs[0], 'grp', split_axis=0, concat_axis=0, tiled=True)  2.98 us
  transfers between devices with their start and end apart: 26, of which 5 were waited for; matrix products, arithmetic and copies ran while one was open for 0% of the time, Pallas kernels for 42%

commit v1 on v0

v1 whole, which is shorter than its diff:
```python
import functools
import math

import jax
import jax.numpy as jnp
from jax import lax
from jax.experimental import pallas as pl
from jax.experimental.pallas import tpu as pltpu
from jax.sharding import PartitionSpec as P


F32 = jnp.float32
BF16 = jnp.bfloat16
LANES = 128
NT = (((1,), (1,)), ((), ()))
TN = (((0,), (0,)), ((), ()))


def call(body, shapes, limit_mib, flops, scratch=(), scalars=(), far=(), args=()):
    spaces = [pltpu.SMEM] * len(scalars) + [pltpu.HBM] * len(far) + [pltpu.VMEM] * len(args)
    far = [pltpu.with_memory_space_constraint(x, pltpu.HBM) for x in far]
    return pl.pallas_call(
        body,
        in_specs=[pl.BlockSpec(memory_space=space) for space in spaces],
        out_specs=[pl.BlockSpec(memory_space=pltpu.VMEM)] * len(shapes),
        out_shape=[jax.ShapeDtypeStruct(*shape) for shape in shapes],
        scratch_shapes=list(scratch),
        compiler_params=pltpu.CompilerParams(vmem_limit_bytes=limit_mib * 2**20),
        cost_estimate=pl.CostEstimate(flops=flops, bytes_accessed=2**20, transcendentals=0),
    )(*scalars, *far, *args)


STRIDE = 40
PARTS = 4


def fetch(source, target, sem):
    copy = pltpu.make_async_copy(source, target, sem)
    copy.start()
    return copy


class Stream:
    def __init__(self, source, target, sems, parts=PARTS, ahead=2):
        size = source.shape[0] // parts
        at = [pl.ds(k * size, size) for k in range(parts)]
        self.copies = [
            pltpu.make_async_copy(source.at[x], target.at[x], sems.at[k])
            for k, x in enumerate(at)
        ]
        self.size = size
        self.started = 0
        self.waited = 0
        self.start(ahead)

    def start(self, count):
        for copy in self.copies[self.started : self.started + count]:
            copy.start()
        self.started = min(len(self.copies), self.started + count)

    def need(self, upto):
        while self.waited * self.size < upto:
            self.copies[self.waited].wait()
            self.waited += 1
            self.start(1)


def three(x):
    top = x.astype(BF16).astype(F32)
    middle = (x - top).astype(BF16).astype(F32)
    return top, middle, x - top - middle


def joined(x, step):
    return x + pltpu.roll(x, LANES - step, 1) + pltpu.roll(x, LANES - 2 * step, 1)


def iota(shape, axis):
    return lax.broadcasted_iota(jnp.int32, shape, axis)


def send_body(me, table_far, ids_far, nope_far, rope_far, *refs, shards, capacity, flips):
    refs = list(refs)
    table, ids, nope, rope, sems = refs[-5:]
    pairs = ((table_far, table), (ids_far, ids), (nope_far, nope), (rope_far, rope))
    copies = [fetch(a, b, sems.at[k]) for k, (a, b) in enumerate(pairs)]
    copies[0].wait()
    copies[1].wait()
    prefixes = table.shape[0]
    requests = ids.shape[1]
    named = ids[...]
    slot = jnp.zeros((1, requests), jnp.int32)
    for p in range(prefixes):
        slot = slot + jnp.where(named == p, table[p], 0)
    hits = (slot == iota((prefixes, requests), 0)).astype(F32)
    before = iota((requests, requests), 0) < iota((requests, requests), 1)
    earlier = jnp.dot(hits, before.astype(F32), preferred_element_type=F32)
    rank = jnp.sum(earlier * hits, axis=0, keepdims=True).astype(jnp.int32)
    each = shards * capacity
    count = prefixes // shards // len(flips)
    row = iota((count * each, requests), 0)
    width = nope.shape[1]
    copies[2].wait()
    copies[3].wait()
    for flip in flips:
        owner = (row // each * len(flips) + flip) ^ me[0]
        pick = (slot == owner * shards + row // capacity % shards) & (rank == row % capacity)
        sel = pick.astype(F32).astype(BF16)
        filled = jnp.sum(pick.astype(F32), axis=1, keepdims=True)
        parts = (
            (0, jnp.dot(sel, nope[...], preferred_element_type=F32)),
            (width, jnp.dot(sel, rope[...], preferred_element_type=F32)),
            (width + rope.shape[1], jnp.broadcast_to(filled, (count * each, LANES))),
        )
        for k in range(count):
            out = refs.pop(0)
            for at, part in parts:
                out[:, at : at + part.shape[1]] = part[k * each : (k + 1) * each].astype(BF16)
        refs.pop(0)[...] = sel


def make_send(me, ids, table, q_nope, q_rope, groups, shards, capacity, flips):
    requests = q_nope.shape[0]
    width = q_nope.shape[1] + q_rope.shape[1] + LANES
    each = shards * capacity
    count = groups // len(flips)
    shapes = ([((each, width), BF16)] * count + [((count * each, requests), BF16)]) * len(flips)
    made = call(
        functools.partial(send_body, shards=shards, capacity=capacity, flips=flips),
        shapes,
        8,
        2 * groups * each * requests * width,
        scratch=[
            pltpu.SMEM(table.shape, jnp.int32),
            pltpu.VMEM((1, requests), jnp.int32),
            pltpu.VMEM(q_nope.shape, BF16),
            pltpu.VMEM(q_rope.shape, BF16),
            pltpu.SemaphoreType.DMA((4,)),
        ],
        scalars=[me],
        far=[table, ids.reshape(1, requests), q_nope, q_rope],
    )
    made = [made[k * (count + 1) : (k + 1) * (count + 1)] for k in range(len(flips))]
    return [x[:count] for x in made], [x[count] for x in made]


def head_place(step, block, j, heads):
    return (j % 2) * (heads // 2) + step * (block // 2) + j // 2


def latent_body(me, nope_far, rope_far, w_uk_far, *refs, shares):
    outs = refs[: sum(shares)]
    q_all, rope_all, nope, rope, w_uk, sems = refs[sum(shares) :]
    copy_rope = fetch(rope_far, rope, sems.at[PARTS])
    copy_nope = fetch(nope_far, nope, sems.at[PARTS + 1])
    stream = Stream(w_uk_far, w_uk, sems)
    requests = nope.shape[0]
    heads, width, wide = w_uk.shape
    blocks = wide // LANES
    half = heads // 2
    copy_rope.wait()
    for j in range(half):
        rope_all[pl.ds(j, requests, stride=half), :] = rope[
            :, j * LANES : (j + 1) * LANES
        ].astype(F32)
    copy_nope.wait()
    for h in range(heads):
        stream.need(h + 1)
        value = jnp.dot(
            nope[:, h * width : (h + 1) * width], w_uk[h], preferred_element_type=F32
        )
        for b in range(blocks):
            q_all[b, pl.ds(head_place(0, heads, h, heads), requests, stride=STRIDE), :] = value[
                :, b * LANES : (b + 1) * LANES
            ]
    share = requests // len(shares)
    outs = list(outs)
    for s, parts in enumerate(shares):
        there = me[0] ^ s
        each = share // parts
        some = each // blocks
        for piece in range(parts):
            ref = outs.pop(0)
            first = there * share + piece * each
            rows = each * heads
            for b in range(blocks):
                lanes = slice(b * LANES, (b + 1) * LANES)
                for r in range(each):
                    base = pl.multiple_of((first + r) * STRIDE, 8)
                    ref[r * heads : (r + 1) * heads, lanes] = q_all[
                        b, pl.ds(base, heads), :
                    ].astype(BF16)
                base = pl.multiple_of((first + b * some) * half, half)
                ref[rows:, lanes] = rope_all[pl.ds(base, some * half), :].astype(BF16)


def latent_queries(me, q_nope, q_rope, w_uk, shares):
    requests = q_nope.shape[0]
    heads, width, wide = w_uk.shape
    share = requests // len(shares)
    shapes = []
    for parts in shares:
        each = share // parts
        rows = each * heads + each * q_rope.shape[1] // wide
        shapes += [((rows, wide), BF16)] * parts
    return call(
        functools.partial(latent_body, shares=shares),
        shapes,
        14,
        4 * requests * heads * width * wide,
        scratch=[
            pltpu.VMEM((wide // LANES, requests * STRIDE, LANES), F32),
            pltpu.VMEM((requests * heads // 2, LANES), F32),
            pltpu.VMEM(q_nope.shape, BF16),
            pltpu.VMEM(q_rope.shape, BF16),
            pltpu.VMEM(w_uk.shape, BF16),
            pltpu.SemaphoreType.DMA((PARTS + 2,)),
        ],
        scalars=[me],
        far=[q_nope, q_rope, w_uk],
    )


TAIL = 16


def suffix_body(me, lengths, cache, keys, *refs, sources, count, first, scale, resident):
    asks, outs = refs[:sources], refs[sources : 2 * sources]
    lse_all, *streamed = refs[2 * sources :]
    share = cache.shape[0]
    wide = asks[0].shape[1]
    dims, tokens = keys.shape[1:]
    heads = asks[0].shape[0] * wide // (count * (wide + dims))
    half = heads // 2
    some = count // (wide // LANES)
    mine = pl.ds(first, count)
    unroll = math.gcd(8, count)
    parts = 2 * count // unroll
    if not resident:
        cache_far, keys_far = cache, keys
        cache, keys, sems, sems_keys = streamed
        stream_keys = Stream(keys_far.at[mine], keys, sems_keys, parts, parts)
        stream = Stream(cache_far.at[mine], cache, sems, parts, parts)
    base = first if resident else 0
    half_lane = iota((half, 2 * dims), 1)
    rows = sources * heads
    position = iota((rows, tokens), 1)
    diag = iota((rows, LANES), 0) == iota((rows, LANES), 1)
    for step in range(count // unroll):
        at = [step * unroll + u for u in range(unroll)]
        scores = []
        for r in at:
            if not resident:
                stream_keys.need(r + 1)
                stream.need(r + 1)
            query = jnp.concatenate([q[r * heads : (r + 1) * heads] for q in asks], axis=0)
            pairs = []
            for ref in asks:
                low = count * heads + (r % some) * half
                pair = ref[low : low + half, r // some * LANES : (r // some + 1) * LANES]
                zero = jnp.zeros_like(pair)
                pairs.append(jnp.where(half_lane < dims, pair, zero))
                pairs.append(jnp.where(half_lane < dims, zero, pair))
            rotary = jnp.concatenate(pairs, axis=0)
            key = keys[base + r]
            both = jnp.concatenate([key, key], axis=0)
            s = lax.dot_general(query, cache[base + r], NT, preferred_element_type=F32)
            s = s + jnp.dot(rotary, both, preferred_element_type=F32)
            length = lengths[me[0] * share + first + r]
            scores.append(jnp.where(position < length, s, F32(-1e30)))
        highest = [jnp.max(s, axis=1, keepdims=True) for s in scores]
        weights = [jnp.exp2((s - m) * scale) for s, m in zip(scores, highest)]
        summed = [jnp.sum(w, axis=1, keepdims=True) for w in weights]
        for r, w, m, total in zip(at, weights, highest, summed):
            value = jnp.dot(w.astype(BF16), cache[base + r], preferred_element_type=F32)
            value = (value * (1.0 / total)).astype(BF16)
            for s in range(sources):
                outs[s][r * heads : (r + 1) * heads, :] = value[s * heads : (s + 1) * heads]
            lse = m * scale + jnp.log2(total)
            lse_all[r : r + 1, :] = jnp.sum(
                jnp.where(diag, lse, F32(0.0)), axis=0, keepdims=True
            )
    if count < TAIL:
        lse_all[count:, :] = jnp.zeros((TAIL - count, LANES), F32)
    lane = iota((TAIL, LANES), 1)
    lse = lse_all[...]
    for s in range(sources):
        x = pltpu.roll(lse, (LANES - s * heads) % LANES, 1)
        top, middle, low = three(jnp.where(lane < heads, x, F32(0.0)))
        x = top + pltpu.roll(middle, heads, 1) + pltpu.roll(low, 2 * heads, 1)
        outs[s][count * heads :, 0:LANES] = x.astype(BF16)
        outs[s][count * heads :, LANES:] = jnp.zeros((TAIL, wide - LANES), BF16)


def suffix_attention(me, lengths, asks, cache, keys, heads, count, first, scale, resident):
    sources = len(asks)
    tokens, wide = cache.shape[1:]
    dims = keys.shape[1]
    parts = 2 * count // math.gcd(8, count)
    scratch = [pltpu.VMEM((TAIL, LANES), F32)]
    if not resident:
        scratch += [
            pltpu.VMEM((count, tokens, wide), BF16),
            pltpu.VMEM((count, dims, tokens), BF16),
            pltpu.SemaphoreType.DMA((parts,)),
            pltpu.SemaphoreType.DMA((parts,)),
        ]
    return call(
        functools.partial(
            suffix_body,
            sources=sources,
            count=count,
            first=first,
            scale=scale,
            resident=resident,
        ),
        [((count * heads + TAIL, wide), BF16)] * sources,
        12,
        2 * sources * heads * count * tokens * (2 * wide + dims) * 4,
        scratch=scratch,
        scalars=[me, lengths],
        far=[] if resident else [cache, keys],
        args=[cache, keys, *asks] if resident else asks,
    )


def owner_body(w_uk, w_uv, latent, keys, *refs, arrays, capacity, sizes, scale):
    pieces, outs = refs[:arrays], refs[arrays : 2 * arrays]
    received, packed, query, both, result = refs[2 * arrays :]
    slots = received.shape[0]
    heads, width, wide = w_uk.shape
    values = w_uv.shape[2]
    shards, dims, tokens = keys.shape
    top_rows = slots // shards
    base = heads * values
    rope_at = heads * width
    both[:, 0:dims] = keys[...]
    both[:, dims:] = keys[...]
    each = slots // arrays
    for k, piece in enumerate(pieces):
        received[k * each : (k + 1) * each, :] = piece[...].astype(received.dtype)
    filled = received[:, rope_at + heads * dims : rope_at + heads * dims + 1].astype(F32)
    here, there = iota((slots, slots), 0), iota((slots, slots), 1)
    filled_row = jnp.sum(jnp.where(here == there, filled, F32(0.0)), axis=0, keepdims=True)
    shard_of = lambda x: x // capacity % shards
    alike = (here < there) & (shard_of(here) == shard_of(there))
    ahead = jnp.sum(jnp.where(alike, filled, F32(0.0)), axis=0, keepdims=True)
    goal = shard_of(there) * top_rows + ahead.astype(jnp.int32)
    move = jnp.where((here == goal) & (filled_row > 0.5), 1.0, 0.0).astype(BF16)
    row_shard = shard_of(iota((1, slots), 1))
    packed[...] = jnp.dot(
        move,
        received[:, 0 : rope_at + heads * dims].astype(BF16),
        preferred_element_type=F32,
    ).astype(BF16)
    result[...] = jnp.zeros(result.shape, BF16)

    def attend(w, rows):
        block = max(2, min(heads, 512 // rows // 2 * 2))
        while heads % block:
            block -= 2
        lane = iota((rows, 2 * dims), 1)
        column = iota((rows, LANES), 1)
        chunk = 512
        mine = pl.ds(pl.multiple_of(w * top_rows, top_rows), rows)

        def some_heads(step, _):
            for j in range(block):
                head = step * block + j
                at = slice(j * rows, (j + 1) * rows)
                nope = packed[mine, pl.ds(pl.multiple_of(head * width, LANES), width)]
                query[at, 0:wide] = jnp.dot(
                    nope, w_uk[head], preferred_element_type=F32
                ).astype(BF16)
                if j % 2 == 0:
                    pair_at = pl.multiple_of(rope_at + head * dims, LANES)
                    pair = packed[mine, pl.ds(pair_at, 2 * dims)]
                keep = (lane < dims) if j % 2 == 0 else (lane >= dims)
                query[at, wide:] = jnp.where(keep, pair, jnp.zeros_like(pair))

            q_latent = query[0 : block * rows, 0:wide]
            q_rotary = query[0 : block * rows, wide:]
            scores = []
            for t in range(0, tokens, chunk):
                s = lax.dot_general(
                    q_latent, latent[w, t : t + chunk, :], NT, preferred_element_type=F32
                )
                scores.append(
                    s + jnp.dot(q_rotary, both[w, :, t : t + chunk], preferred_element_type=F32)
                )
            highest = functools.reduce(
                jnp.maximum, [jnp.max(s, axis=1, keepdims=True) for s in scores]
            )
            summed = None
            mixed = None
            for s, t in zip(scores, range(0, tokens, chunk)):
                weights = jnp.exp2((s - highest) * scale)
                total = jnp.sum(weights, axis=1, keepdims=True)
                product = jnp.dot(
                    weights.astype(BF16), latent[w, t : t + chunk, :], preferred_element_type=F32
                )
                summed = total if summed is None else summed + total
                mixed = product if mixed is None else mixed + product
            mixed = (mixed * (1.0 / summed)).astype(BF16)
            lse = highest * scale + jnp.log2(summed)
            tail = jnp.zeros((rows, LANES), F32)
            for j in range(block):
                at = slice(j * rows, (j + 1) * rows)
                head = step * block + j
                value = jnp.dot(mixed[at], w_uv[head], preferred_element_type=F32)
                result[mine, pl.ds(pl.multiple_of(head * values, LANES), values)] = value.astype(
                    BF16
                )
                top, middle, low = three(lse[at])
                place = head_place(step, block, j, heads)
                tail = jnp.where(column == place, top, tail)
                tail = jnp.where(column == heads + place, middle, tail)
                tail = jnp.where(column == 2 * heads + place, low, tail)
            result[mine, base:] = (result[mine, base:].astype(F32) + tail).astype(BF16)
            return 0

        lax.fori_loop(0, heads // block, some_heads, 0)

    def one_shard(w, _):
        count = jnp.sum(jnp.where(row_shard == w, filled_row, F32(0.0))).astype(jnp.int32)
        for low, high in zip((-1,) + sizes[:-1], sizes):
            pl.when((count > low) & (count <= high))(functools.partial(attend, w, high))
        return 0

    lax.fori_loop(0, shards, one_shard, 0)
    answer = lax.dot_general(move, result[...], TN, preferred_element_type=F32)
    for k, out in enumerate(outs):
        out[...] = answer[k * each : (k + 1) * each].astype(BF16)


def owner_attention(received, w_uk, w_uv, latent, keys, capacity, scale):
    arrays = len(received)
    each = received[0].shape[0]
    slots = arrays * each
    heads, width, wide = w_uk.shape
    values = w_uv.shape[2]
    shards, tokens = latent.shape[:2]
    dims = keys.shape[1]
    top = slots // shards
    sizes = tuple(x for x in (16, 24) if x < top) + (top,)
    return call(
        functools.partial(
            owner_body, arrays=arrays, capacity=capacity, sizes=sizes, scale=scale
        ),
        [((each, heads * values + LANES), BF16)] * arrays,
        20,
        2 * heads * slots * tokens * (2 * wide + dims),
        scratch=[
            pltpu.VMEM((slots, received[0].shape[1]), BF16 if each % 16 == 0 else F32),
            pltpu.VMEM((slots, heads * (width + dims)), BF16),
            pltpu.VMEM((max(512, 2 * top), wide + 2 * dims), BF16),
            pltpu.VMEM((shards, 2 * dims, tokens), BF16),
            pltpu.VMEM((slots, heads * values + LANES), BF16),
        ],
        args=[w_uk, w_uv, latent, keys, *received],
    )


def project_body(me, w_uv, *refs, shares):
    tells = list(refs[: sum(shares)])
    out, lse_out, s_all = refs[sum(shares) :]
    heads, wide, values = w_uv.shape
    requests = out.shape[0]
    blocks = wide // LANES
    share = requests // len(shares)
    for s, parts in enumerate(shares):
        there = me[0] ^ s
        each = share // parts
        for piece in range(parts):
            ref = tells.pop(0)
            first = there * share + piece * each
            rows = each * heads
            for b in range(blocks):
                for r in range(each):
                    base = pl.multiple_of((first + r) * STRIDE, 8)
                    part = ref[r * heads : (r + 1) * heads, b * LANES : (b + 1) * LANES]
                    s_all[b, pl.ds(base, heads), :] = part.astype(F32)
            lse = joined(ref[rows:, 0:LANES].astype(F32), heads)
            lse_out[pl.ds(pl.multiple_of(first, each), each), :] = lse[0:each]
    for h in range(heads):
        place = head_place(0, heads, h, heads)
        rows = [
            s_all[b, pl.ds(place, requests, stride=STRIDE), :].astype(BF16) for b in range(blocks)
        ]
        value = jnp.dot(jnp.concatenate(rows, axis=1), w_uv[h], preferred_element_type=F32)
        out[:, h * values : (h + 1) * values] = value.astype(BF16)


def project(me, tells, w_uv, requests, shares):
    heads, wide, values = w_uv.shape
    return call(
        functools.partial(project_body, shares=shares),
        [((requests, heads * values), BF16), ((requests, LANES), F32)],
        14,
        4 * requests * heads * wide * values,
        scratch=[
            pltpu.VMEM((wide // LANES, requests * STRIDE, LANES), F32),
        ],
        scalars=[me],
        args=[w_uv, *tells],
    )


def mix_body(*refs, arrays, heads):
    refs = list(refs)
    places = [refs.pop(0) for _ in arrays]
    backs = [[refs.pop(0) for _ in range(n)] for n in arrays]
    suffix, lse_s, out = refs[:3]
    scratches = refs[3:]
    values = out.shape[1] // heads
    for parts, scratch in zip(backs, scratches):
        each = parts[0].shape[0]
        for k, part in enumerate(parts):
            scratch[k * each : (k + 1) * each, :] = part[...].astype(scratch.dtype)

    def gather(lo, hi):
        found = [
            lax.dot_general(p[...], b[:, lo:hi].astype(BF16), TN, preferred_element_type=F32)
            for p, b in zip(places, scratches)
        ]
        return functools.reduce(jnp.add, found)

    lse_p = joined(gather(heads * values, heads * values + LANES), heads)
    lse_s = lse_s[...]
    overall = jnp.maximum(lse_p, lse_s)
    a = jnp.exp2(lse_p - overall)
    b = jnp.exp2(lse_s - overall)
    total = 1.0 / (a + b)
    a = a * total
    b = b * total
    some = 4
    for first in range(0, heads, some):
        prefix = gather(first * values, (first + some) * values)
        for h in range(first, first + some):
            place = head_place(0, heads, h, heads)
            at = slice(h * values, (h + 1) * values)
            mine = prefix[:, (h - first) * values : (h - first + 1) * values]
            mixed = (
                a[:, place : place + 1] * mine
                + b[:, place : place + 1] * suffix[:, at].astype(F32)
            )
            out[:, at] = mixed.astype(BF16)


def mix(places, backs, suffix, lse, heads):
    requests, width = suffix.shape
    arrays = tuple(len(parts) for parts in backs)
    rows = places[0].shape[0]
    kind = BF16 if backs[0][0].shape[0] % 16 == 0 else F32
    return call(
        functools.partial(mix_body, arrays=arrays, heads=heads),
        [((requests, width), BF16)],
        8,
        2 * requests * rows * width,
        scratch=[pltpu.VMEM((rows, width + LANES), kind)] * len(arrays),
        args=[*places, *[x for parts in backs for x in parts], suffix, lse],
    )[0]


def local(
    q_nope,
    q_rope,
    w_uk,
    w_uv,
    prefix_latent,
    prefix_rope,
    suffix_latent,
    suffix_rope,
    suffix_len,
    request_prefix,
    prefix_slot,
):
    groups = lax.axis_size("grp")
    ranks = lax.axis_size("tp")
    requests = q_nope.shape[0]
    prefixes = prefix_slot.shape[0]
    shards = prefix_latent.shape[0]
    capacity = max(2, 2 * requests // prefixes)
    scale = math.log2(math.e) / math.sqrt(w_uk.shape[1] + prefix_rope.shape[1])
    share = requests // ranks
    heads = w_uk.shape[0]
    near, pieces = min(2, ranks), 1
    shares = (1,) * near + (pieces,) * (ranks - near)
    flips = tuple(range(min(2, groups)))
    mine = lax.axis_index("grp").astype(jnp.int32).reshape(1)
    me = lax.axis_index("tp").astype(jnp.int32).reshape(1)
    lengths = suffix_len.reshape(-1)

    def swap(x, s, axis, size):
        if s == 0:
            return x
        return lax.ppermute(x, axis, [(k, k ^ s) for k in range(size)])

    def exchange(xs, flip):
        last = len(flips)
        return [swap(x, d * last + flip, "grp", groups) for d, x in enumerate(xs)]

    sends, places = make_send(
        mine, request_prefix, prefix_slot, q_nope, q_rope, groups, shards, capacity, flips
    )
    order = flips
    received = {flip: exchange(sends[flip], flip) for flip in order}

    made = list(latent_queries(me, q_nope, q_rope, w_uk, shares))
    asks = [
        [swap(made.pop(0), s, "tp", ranks) for _ in range(parts)]
        for s, parts in enumerate(shares)
    ]

    def attend(some, p, count, resident):
        return suffix_attention(
            me,
            lengths,
            [asks[s][p] for s in some],
            suffix_latent,
            suffix_rope,
            heads,
            count,
            p * count,
            scale,
            resident,
        )

    tells = [[None] * parts for parts in shares]
    for s, x in enumerate(attend(range(near), 0, share, True)):
        tells[s][0] = swap(x, s, "tp", ranks)
    for p in range(pieces):
        for s, x in enumerate(attend(range(near, ranks), p, share // pieces, True), near):
            tells[s][p] = swap(x, s, "tp", ranks)

    backs = {}
    for flip in order:
        result = owner_attention(
            received[flip], w_uk, w_uv, prefix_latent, prefix_rope, capacity, scale
        )
        backs[flip] = exchange(result, flip)
    suffix, lse = project(me, [x for parts in tells for x in parts], w_uv, requests, shares)
    return mix(places, [backs[flip] for flip in flips], suffix, lse, heads)


def solution(mesh):
    in_specs = (
        P("grp", "tp"),
        P("grp", "tp"),
        P("tp", None, None),
        P("tp", None, None),
        P("grp", None, None),
        P("grp", None, None),
        P(("grp", "tp"), None, None),
        P(("grp", "tp"), None, None),
        P("grp", None),
        P("grp"),
        P(),
    )

    return jax.shard_map(
        local, mesh=mesh, in_specs=in_specs, out_specs=P("grp", "tp"), check_vma=False
    )
```

time: 122 us -> 99.3 us (0.81)
  Pallas kernels: 54.8 us -> 37.3 us
  starting transfers between devices: 39.6 us -> 35.9 us
    pallas_call x9 -> x8, Pallas kernels: 54.8 us -> 37.3 us  [call(): pl.pallas_call(body, in_specs=[pl.BlockSpec(memory_space=space) for space...]
    all_to_all x2 -> x0, starting transfers between devices: 10.8 us -> none  [exchange(): lax.all_to_all(xs[0], 'grp', split_axis=0, concat_axis=0, tiled=True)]
    ppermute x24 -> x20, starting transfers between devices: 28.7 us -> 35.9 us  [swap(): return lax.ppermute(x, axis, [(k, k ^ s) for k in range(size)])]
    all_to_all x2 -> x0, waiting for transfers between devices: 2.98 us -> none  [exchange(): lax.all_to_all(xs[0], 'grp', split_axis=0, concat_axis=0, tiled=True)]
    ppermute x24 -> x20, waiting for transfers between devices: 18.1 us -> 20.8 us  [swap(): return lax.ppermute(x, axis, [(k, k ^ s) for k in range(size)])]
  transfers between devices with their start and end apart: 26 -> 20, of which waited for: 5 -> 5; matrix products, arithmetic and copies ran while one was open for 0% -> 0% of each run, Pallas kernels for 42% -> 34%
where the time goes in v1:
time: 99.3 us; the launch traced here: 98.4 us
  Pallas kernels  37.3 us (38%)
  starting transfers between devices  35.9 us (36%)
  waiting for transfers between devices  20.8 us (21%)
  local copies, waits for them, and re-layouts  4.41 us (4%)
    pallas_call x8, Pallas kernels, call(): pl.pallas_call(body, in_specs=[pl.BlockSpec(memory_space=space) for space...  37.3 us
    ppermute x20, starting transfers between devices, swap(): return lax.ppermute(x, axis, [(k, k ^ s) for k in range(size)])  35.9 us
    ppermute x20, waiting for transfers between devices, swap(): return lax.ppermute(x, axis, [(k, k ^ s) for k in range(size)])  20.8 us
    unnamed x18, local copies, waits for them, and re-layouts  4.41 us
  transfers between devices with their start and end apart: 20, of which 5 were waited for; matrix products, arithmetic and copies ran while one was open for 0% of the time, Pallas kernels for 34%

profile of v1, /device:TPU:0, one launch (start us, length us, event | category | flops | bytes accessed | tf_op | source)
XLA Modules:
  0.0 98.4 jit_solution(14607901223844959504)
XLA Ops:
  0.0 1.8 %shard_map.109 = (bf16[16,6272]{1,0:T(8,128)(2,1)S(1)}, bf16[16,6272]{1,0:T(8,128)(2,1)S(1)}, bf16[16,6272]{1,0:T(8,128)(2,1)S(1)}, bf16[16,6272]{1,0:T(8,128)(2...) custom-call(s32[1]{0:T(128)} %bitcast.me, ...), custom_call_target="tpu_custom_call" | custom-call | flops 102760448 | bytes 1048576 | tf_op jit(solution)/shard_map/pallas_call | solution.py:22
  1.8 3.0 %collective-permute-start.6 = (bf16[16,6272]{1,0:T(8,128)(2,1)S(1)}, bf16[16,6272]{1,0:T(8,128)(2,1)S(1)}, u32[]{:S(2)}, u32[]{:S(2)}) collective-permute-start(bf16[16,6272]{1,0:T(8,128)(2,1)S(1)} %get-tuple-element.43), channel_id=1, source_target_pairs={{0,4},{4,0},{8,12},{12,8},{16,20},{20,16},{24,28},{28,24},{1,5},{5... | collective-permute-start | bytes 602120 | tf_op jit(solution)/shard_map/ppermute | solution.py:597
  6.4 3.5 %collective-permute-start.8 = (bf16[16,6272]{1,0:T(8,128)(2,1)S(1)}, bf16[16,6272]{1,0:T(8,128)(2,1)S(1)}, u32[]{:S(2)}, u32[]{:S(2)}) collective-permute-start(bf16[16,6272]{1,0:T(8,128)(2,1)S(1)} %get-tuple-element.45), channel_id=1, source_target_pairs={{0,20},{4,16},{8,28},{12,24},{16,4},{20,0},{24,12},{28,8},{1,21},{... | collective-permute-start | bytes 602120 | tf_op jit(solution)/shard_map/ppermute | solution.py:597
  9.9 4.3 %shard_map.112 = (bf16[576,512]{1,0:T(8,128)(2,1)S(1)}, bf16[576,512]{1,0:T(8,128)(2,1)S(1)}, bf16[576,512]{1,0:T(8,128)(2,1)S(1)}, bf16[576,512]{1,0:T(8,128)(2,1)S(1)}) custom-call(s32[1]{0:T(128)} %bitcast.2.me, bf16[64,4096]{1,0:T(8,128)(2,1)} %nope_far.3, bf16[64,2048]{1,0:T(8,128)(2,1)} %rope_far.3, bf16[32,128,512]{2,1,0:T(8,128)(2,1)} %w_uk_far.1), custom_call_target="tpu_custom_call" | custom-call | flops 536870912 | bytes 1048576 | tf_op jit(solution)/shard_map/pallas_call | solution.py:22
  14.2 1.8 %collective-permute-start.16 = (bf16[576,512]{1,0:T(8,128)(2,1)S(1)}, bf16[576,512]{1,0:T(8,128)(2,1)S(1)}, u32[]{:S(2)}, u32[]{:S(2)}) collective-permute-start(bf16[576,512]{1,0:T(8,128)(2,1)S(1)} %get-tuple-element.55), channel_id=1, source_target_pairs={{0,2},{1,3},{2,0},{3,1},{4,6},{5,7},{6,4},{7,5},{8,10},{9,11},{10,... | collective-permute-start | bytes 1769480 | tf_op jit(solution)/shard_map/ppermute | solution.py:597
  15.9 1.8 %collective-permute-done.6.refs_0_ = bf16[16,6272]{1,0:T(8,128)(2,1)S(1)} collective-permute-done((bf16[16,6272]{1,0:T(8,128)(2,1)S(1)}, bf16[16,6272]{1,0:T(8,128)(2,1)S(1)}, u32[]{:S(2)}, u32[]{:S(2)}) %collective-permute-start.6) | collective-permute-done | bytes 200736 | tf_op jit(solution)/shard_map/ppermute | solution.py:597
  17.9 2.0 %collective-permute-start.14 = (bf16[576,512]{1,0:T(8,128)(2,1)S(1)}, bf16[576,512]{1,0:T(8,128)(2,1)S(1)}, u32[]{:S(2)}, u32[]{:S(2)}) collective-permute-start(bf16[576,512]{1,0:T(8,128)(2,1)S(1)} %get-tuple-element.52), channel_id=1, source_target_pairs={{0,1},{1,0},{2,3},{3,2},{4,5},{5,4},{6,7},{7,6},{8,9},{9,8},{10,11... | collective-permute-start | bytes 1769480 | tf_op jit(solution)/shard_map/ppermute | solution.py:597
  19.9 4.8 %collective-permute-done.8.refs_2_ = bf16[16,6272]{1,0:T(8,128)(2,1)S(1)} collective-permute-done((bf16[16,6272]{1,0:T(8,128)(2,1)S(1)}, bf16[16,6272]{1,0:T(8,128)(2,1)S(1)}, u32[]{:S(2)}, u32[]{:S(2)}) %collective-permute-start.8) | collective-permute-done | bytes 200736 | tf_op jit(solution)/shard_map/ppermute | solution.py:597
  24.7 4.4 %collective-permute-start.1 = (bf16[16,6272]{1,0:T(8,128)(2,1)S(1)}, bf16[16,6272]{1,0:T(8,128)(2,1)S(1)}, u32[]{:S(2)}, u32[]{:S(2)}) collective-permute-start(bf16[16,6272]{1,0:T(8,128)(2,1)S(1)} %get-tuple-element.37), channel_id=1, source_target_pairs={{0,16},{4,20},{8,24},{12,28},{16,0},{20,4},{24,8},{28,12},{1,17},{... | collective-permute-start | bytes 602120 | tf_op jit(solution)/shard_map/ppermute | solution.py:597
  29.1 2.2 %copy-done.1 = bf16[32,512,128]{2,1,0:T(8,128)(2,1)S(1)} copy-done((bf16[32,512,128]{2,1,0:T(8,128)(2,1)S(1)}, bf16[32,512,128]{2,1,0:T(8,128)(2,1)}, u32[]{:S(2)}) %copy-start.1) | copy-done | bytes 4194328
  31.3 2.2 %copy-done.4 = bf16[2,2048,512]{2,1,0:T(8,128)(2,1)S(1)} copy-done((bf16[2,2048,512]{2,1,0:T(8,128)(2,1)S(1)}, bf16[2,2048,512]{2,1,0:T(8,128)(2,1)}, u32[]{:S(2)}) %copy-start.4) | copy-done | bytes 4194328
  33.5 10.0 %shard_map.111 = (bf16[16,4224]{1,0:T(8,128)(2,1)S(1)}, bf16[16,4224]{1,0:T(8,128)(2,1)S(1)}, bf16[16,4224]{1,0:T(8,128)(2,1)S(1)}, bf16[16,4224]{1,0:T(8,128)(2,1)S(1)}) custom-call(bf16[32,128,512]{2,1,0:T(8,128)(2,1)S(1)} %copy-done, bf16[32,512,128]{2,1,0:T(8,128)(2,1)S(1)} %copy-done.1, bf16[2,2048,512]{2,1,0:T(8,128)(2,1)S(1)} %copy-done.4, ...), custom_call_target="tpu_custom_call" | custom-call | flops 9126805504 | bytes 1048576 | tf_op jit(solution)/shard_map/pallas_call | solution.py:22
  44.8 5.4 %collective-permute-start.10 = (bf16[16,4224]{1,0:T(8,128)(2,1)S(1)}, bf16[16,4224]{1,0:T(8,128)(2,1)S(1)}, u32[]{:S(2)}, u32[]{:S(2)}) collective-permute-start(bf16[16,4224]{1,0:T(8,128)(2,1)S(1)} %get-tuple-element.47), channel_id=1, source_target_pairs={{0,4},{4,0},{8,12},{12,8},{16,20},{20,16},{24,28},{28,24},{1,5},{5... | collective-permute-start | bytes 405512 | tf_op jit(solution)/shard_map/ppermute | solution.py:597
  50.3 3.0 %shard_map.114 = (bf16[528,512]{1,0:T(8,128)(2,1)S(1)}, bf16[528,512]{1,0:T(8,128)(2,1)S(1)}) custom-call(s32[1]{0:T(128)} %bitcast.2.me, s32[64]{0:T(128)S(1)} %bitcast.4, bf16[16,256,512]{2,1,0:T(8,128)(2,1)S(1)} %copy-done.3, bf16[16,64,256]{2,1,0:T(8,128)(2,1)S(1)} %copy-done.6, bf16[576,512]{1,0:T(8,128)(2,1)S(1)} %collective-permute-done.16.refs_0_, ...), custom_call_target="tpu_custom_call" | custom-call | flops 2281701376 | bytes 1048576 | tf_op jit(solution)/shard_map/pallas_call | solution.py:22
  53.3 3.0 %shard_map.113 = (bf16[528,512]{1,0:T(8,128)(2,1)S(1)}, bf16[528,512]{1,0:T(8,128)(2,1)S(1)}) custom-call(s32[1]{0:T(128)} %bitcast.2.me, s32[64]{0:T(128)S(1)} %bitcast.5, bf16[16,256,512]{2,1,0:T(8,128)(2,1)S(1)} %copy-done.3, bf16[16,64,256]{2,1,0:T(8,128)(2,1)S(1)} %copy-done.6, bf16[576,512]{1,0:T(8,128)(2,1)S(1)} %get-tuple-element.51.refs_0_, ...), custom_call_target="tpu_custom_call" | custom-call | flops 2281701376 | bytes 1048576 | tf_op jit(solution)/shard_map/pallas_call | solution.py:22
  58.4 12.0 %shard_map.110 = (bf16[16,4224]{1,0:T(8,128)(2,1)S(1)}, bf16[16,4224]{1,0:T(8,128)(2,1)S(1)}, bf16[16,4224]{1,0:T(8,128)(2,1)S(1)}, bf16[16,4224]{1,0:T(8,128)(2,1)S(1)}) custom-call(bf16[32,128,512]{2,1,0:T(8,128)(2,1)S(1)} %copy-done, bf16[32,512,128]{2,1,0:T(8,128)(2,1)S(1)} %copy-done.2, bf16[2,2048,512]{2,1,0:T(8,128)(2,1)S(1)} %copy-done.5, ...), custom_call_target="tpu_custom_call" | custom-call | flops 9126805504 | bytes 1048576 | tf_op jit(solution)/shard_map/pallas_call | solution.py:22
  70.4 3.3 %collective-permute-start.12 = (bf16[16,4224]{1,0:T(8,128)(2,1)S(1)}, bf16[16,4224]{1,0:T(8,128)(2,1)S(1)}, u32[]{:S(2)}, u32[]{:S(2)}) collective-permute-start(bf16[16,4224]{1,0:T(8,128)(2,1)S(1)} %get-tuple-element.49), channel_id=1, source_target_pairs={{0,20},{4,16},{8,28},{12,24},{16,4},{20,0},{24,12},{28,8},{1,21},{... | collective-permute-start | bytes 405512 | tf_op jit(solution)/shard_map/ppermute | solution.py:597
  73.7 3.5 %collective-permute-start.13 = (bf16[16,4224]{1,0:T(8,128)(2,1)S(1)}, bf16[16,4224]{1,0:T(8,128)(2,1)S(1)}, u32[]{:S(2)}, u32[]{:S(2)}) collective-permute-start(bf16[16,4224]{1,0:T(8,128)(2,1)S(1)} %get-tuple-element.50), channel_id=1, source_target_pairs={{0,28},{4,24},{8,20},{12,16},{16,12},{20,8},{24,4},{28,0},{1,29},{... | collective-permute-start | bytes 405512 | tf_op jit(solution)/shard_map/ppermute | solution.py:597
  77.2 2.2 %collective-permute-done.19.refs_3_ = bf16[528,512]{1,0:T(8,128)(2,1)S(1)} collective-permute-done((bf16[528,512]{1,0:T(8,128)(2,1)S(1)}, bf16[528,512]{1,0:T(8,128)(2,1)S(1)}, u32[]{:S(2)}, u32[]{:S(2)}) %collective-permute-start.19) | collective-permute-done | bytes 540704 | tf_op jit(solution)/shard_map/ppermute | solution.py:597
  79.3 3.4 %collective-permute-start.4 = (bf16[16,4224]{1,0:T(8,128)(2,1)S(1)}, bf16[16,4224]{1,0:T(8,128)(2,1)S(1)}, u32[]{:S(2)}, u32[]{:S(2)}) collective-permute-start(bf16[16,4224]{1,0:T(8,128)(2,1)S(1)} %get-tuple-element.41), channel_id=1, source_target_pairs={{0,16},{4,20},{8,24},{12,28},{16,0},{20,4},{24,8},{28,12},{1,17},{... | collective-permute-start | bytes 405512 | tf_op jit(solution)/shard_map/ppermute | solution.py:597
  83.1 1.6 %shard_map.115 = (bf16[64,4096]{1,0:T(8,128)(2,1)S(1)}, f32[64,128]{1,0:T(8,128)S(1)}) custom-call(s32[1]{0:T(128)} %bitcast.2.me, bf16[32,512,128]{2,1,0:T(8,128)(2,1)S(1)} %copy-done.2, bf16[528,512]{1,0:T(8,128)(2,1)S(1)} %get-tuple-element.53.refs_0_, bf16[528,512]{1,0:T(8,128)(2,1)S(1)} %collective-permute-done.15.refs_1_, ...), custom_call_target="tpu_custom_call" | custom-call | flops 536870912 | bytes 1048576 | tf_op jit(solution)/shard_map/pallas_call | solution.py:22
  84.7 3.1 %collective-permute-done.3.refs_3_ = bf16[16,4224]{1,0:T(8,128)(2,1)S(1)} collective-permute-done((bf16[16,4224]{1,0:T(8,128)(2,1)S(1)}, bf16[16,4224]{1,0:T(8,128)(2,1)S(1)}, u32[]{:S(2)}, u32[]{:S(2)}) %collective-permute-start.3) | collective-permute-done | bytes 135200 | tf_op jit(solution)/shard_map/ppermute | solution.py:597
  87.8 8.9 %collective-permute-done.4.refs_4_ = bf16[16,4224]{1,0:T(8,128)(2,1)S(1)} collective-permute-done((bf16[16,4224]{1,0:T(8,128)(2,1)S(1)}, bf16[16,4224]{1,0:T(8,128)(2,1)S(1)}, u32[]{:S(2)}, u32[]{:S(2)}) %collective-permute-start.4) | collective-permute-done | bytes 135200 | tf_op jit(solution)/shard_map/ppermute | solution.py:597
  96.7 1.8 %shard_map.116 = bf16[64,4096]{1,0:T(8,128)(2,1)} custom-call(bf16[64,64]{1,0:T(8,128)(2,1)S(1)} %get-tuple-element.33.refs_0_, bf16[64,64]{1,0:T(8,128)(2,1)S(1)} %get-tuple-element.34.refs_1_, bf16[16,4224]{1,0:T(8,128)(2,1)S(1)} %get-tuple-element.39.refs_2_, bf16[16,4224]{1,0:T(8,128)(2,1)S(1)} %collective-permute-done.3.refs_3_, ...), custom_call_target="tpu_custom_call" | custom-call | flops 33554432 | bytes 1048576 | tf_op jit(solution)/shard_map/pallas_call | solution.py:22
  (42 shorter events, 5.6 us)
Async XLA Ops:
  0.0 29.1 %copy-start.7 = (bf16[2,64,2048]{2,1,0:T(8,128)(2,1)S(1)}, bf16[2,64,2048]{2,1,0:T(8,128)(2,1)}, u32[]{:S(2)}) copy-start(bf16[2,64,2048]{2,1,0:T(8,128)(2,1)} %keys.5) | copy-start | bytes 1572868
  1.8 16.0 %collective-permute-start.6 = (bf16[16,6272]{1,0:T(8,128)(2,1)S(1)}, bf16[16,6272]{1,0:T(8,128)(2,1)S(1)}, u32[]{:S(2)}, u32[]{:S(2)}) collective-permute-start(bf16[16,6272]{1,0:T(8,128)(2,1)S(1)} %get-tuple-element.43), channel_id=1, source_target_pairs={{0,4},{4,0},{8,12},{12,8},{16,20},{20,16},{24,28},{28,24},{1,5},{5... | collective-permute-start | bytes 602120 | tf_op jit(solution)/shard_map/ppermute | solution.py:597
  4.8 13.1 %collective-permute-start.7 = (bf16[16,6272]{1,0:T(8,128)(2,1)S(1)}, bf16[16,6272]{1,0:T(8,128)(2,1)S(1)}, u32[]{:S(2)}, u32[]{:S(2)}) collective-permute-start(bf16[16,6272]{1,0:T(8,128)(2,1)S(1)} %get-tuple-element.44), channel_id=1, source_target_pairs={{0,12},{4,8},{8,4},{12,0},{16,28},{20,24},{24,20},{28,16},{1,13},{... | collective-permute-start | bytes 602120 | tf_op jit(solution)/shard_map/ppermute | solution.py:597
  6.4 18.3 %collective-permute-start.8 = (bf16[16,6272]{1,0:T(8,128)(2,1)S(1)}, bf16[16,6272]{1,0:T(8,128)(2,1)S(1)}, u32[]{:S(2)}, u32[]{:S(2)}) collective-permute-start(bf16[16,6272]{1,0:T(8,128)(2,1)S(1)} %get-tuple-element.45), channel_id=1, source_target_pairs={{0,20},{4,16},{8,28},{12,24},{16,4},{20,0},{24,12},{28,8},{1,21},{... | collective-permute-start | bytes 602120 | tf_op jit(solution)/shard_map/ppermute | solution.py:597
  9.9 14.8 %collective-permute-start.9 = (bf16[16,6272]{1,0:T(8,128)(2,1)S(1)}, bf16[16,6272]{1,0:T(8,128)(2,1)S(1)}, u32[]{:S(2)}, u32[]{:S(2)}) collective-permute-start(bf16[16,6272]{1,0:T(8,128)(2,1)S(1)} %get-tuple-element.46), channel_id=1, source_target_pairs={{0,28},{4,24},{8,20},{12,16},{16,12},{20,8},{24,4},{28,0},{1,29},{... | collective-permute-start | bytes 602120 | tf_op jit(solution)/shard_map/ppermute | solution.py:597
  9.9 19.2 %copy-start = (bf16[32,128,512]{2,1,0:T(8,128)(2,1)S(1)}, bf16[32,128,512]{2,1,0:T(8,128)(2,1)}, u32[]{:S(2)}) copy-start(bf16[32,128,512]{2,1,0:T(8,128)(2,1)} %w_uk_far.1) | copy-start | bytes 12582916
  14.2 29.4 %collective-permute-start.16 = (bf16[576,512]{1,0:T(8,128)(2,1)S(1)}, bf16[576,512]{1,0:T(8,128)(2,1)S(1)}, u32[]{:S(2)}, u32[]{:S(2)}) collective-permute-start(bf16[576,512]{1,0:T(8,128)(2,1)S(1)} %get-tuple-element.55), channel_id=1, source_target_pairs={{0,2},{1,3},{2,0},{3,1},{4,6},{5,7},{6,4},{7,5},{8,10},{9,11},{10,... | collective-permute-start | bytes 1769480 | tf_op jit(solution)/shard_map/ppermute | solution.py:597
  17.8 27.0 %collective-permute-start.17 = (bf16[576,512]{1,0:T(8,128)(2,1)S(1)}, bf16[576,512]{1,0:T(8,128)(2,1)S(1)}, u32[]{:S(2)}, u32[]{:S(2)}) collective-permute-start(bf16[576,512]{1,0:T(8,128)(2,1)S(1)} %get-tuple-element.56), channel_id=1, source_target_pairs={{0,3},{1,2},{2,1},{3,0},{4,7},{5,6},{6,5},{7,4},{8,11},{9,10},{10,... | collective-permute-start | bytes 1769480 | tf_op jit(solution)/shard_map/ppermute | solution.py:597
  17.9 35.3 %collective-permute-start.14 = (bf16[576,512]{1,0:T(8,128)(2,1)S(1)}, bf16[576,512]{1,0:T(8,128)(2,1)S(1)}, u32[]{:S(2)}, u32[]{:S(2)}) collective-permute-start(bf16[576,512]{1,0:T(8,128)(2,1)S(1)} %get-tuple-element.52), channel_id=1, source_target_pairs={{0,1},{1,0},{2,3},{3,2},{4,5},{5,4},{6,7},{7,6},{8,9},{9,8},{10,11... | collective-permute-start | bytes 1769480 | tf_op jit(solution)/shard_map/ppermute | solution.py:597
  24.7 31.6 %collective-permute-start = (bf16[16,6272]{1,0:T(8,128)(2,1)S(1)}, bf16[16,6272]{1,0:T(8,128)(2,1)S(1)}, u32[]{:S(2)}, u32[]{:S(2)}) collective-permute-start(bf16[16,6272]{1,0:T(8,128)(2,1)S(1)} %get-tuple-element.36), channel_id=1, source_target_pairs={{0,8},{4,12},{8,0},{12,4},{16,24},{20,28},{24,16},{28,20},{1,9},{5... | collective-permute-start | bytes 602120 | tf_op jit(solution)/shard_map/ppermute | solution.py:597
  24.7 33.1 %collective-permute-start.1 = (bf16[16,6272]{1,0:T(8,128)(2,1)S(1)}, bf16[16,6272]{1,0:T(8,128)(2,1)S(1)}, u32[]{:S(2)}, u32[]{:S(2)}) collective-permute-start(bf16[16,6272]{1,0:T(8,128)(2,1)S(1)} %get-tuple-element.37), channel_id=1, source_target_pairs={{0,16},{4,20},{8,24},{12,28},{16,0},{20,4},{24,8},{28,12},{1,17},{... | collective-permute-start | bytes 602120 | tf_op jit(solution)/shard_map/ppermute | solution.py:597
  33.5 16.8 %copy-start.6 = (bf16[16,64,256]{2,1,0:T(8,128)(2,1)S(1)}, bf16[16,64,256]{2,1,0:T(8,128)(2,1)}, u32[]{:S(2)}) copy-start(bf16[16,64,256]{2,1,0:T(8,128)(2,1)} %keys.7) | copy-start | bytes 1572868
  33.5 16.8 %copy-start.8 = (s32[1,64]{1,0:T(1,128)S(1)}, s32[1,64]{1,0:T(1,128)}, u32[]{:S(2)}) copy-start(s32[1,64]{1,0:T(1,128)} %param.19) | copy-start | bytes 772
  43.5 14.3 %collective-permute-start.2 = (bf16[16,6272]{1,0:T(8,128)(2,1)S(1)}, bf16[16,6272]{1,0:T(8,128)(2,1)S(1)}, u32[]{:S(2)}, u32[]{:S(2)}) collective-permute-start(bf16[16,6272]{1,0:T(8,128)(2,1)S(1)} %get-tuple-element.38), channel_id=1, source_target_pairs={{0,24},{4,28},{8,16},{12,20},{16,8},{20,12},{24,0},{28,4},{1,25},{... | collective-permute-start | bytes 602120 | tf_op jit(solution)/shard_map/ppermute | solution.py:597
  44.8 25.6 %collective-permute-start.10 = (bf16[16,4224]{1,0:T(8,128)(2,1)S(1)}, bf16[16,4224]{1,0:T(8,128)(2,1)S(1)}, u32[]{:S(2)}, u32[]{:S(2)}) collective-permute-start(bf16[16,4224]{1,0:T(8,128)(2,1)S(1)} %get-tuple-element.47), channel_id=1, source_target_pairs={{0,4},{4,0},{8,12},{12,8},{16,20},{20,16},{24,28},{28,24},{1,5},{5... | collective-permute-start | bytes 405512 | tf_op jit(solution)/shard_map/ppermute | solution.py:597
  53.2 20.5 %collective-permute-start.11 = (bf16[16,4224]{1,0:T(8,128)(2,1)S(1)}, bf16[16,4224]{1,0:T(8,128)(2,1)S(1)}, u32[]{:S(2)}, u32[]{:S(2)}) collective-permute-start(bf16[16,4224]{1,0:T(8,128)(2,1)S(1)} %get-tuple-element.48), channel_id=1, source_target_pairs={{0,12},{4,8},{8,4},{12,0},{16,28},{20,24},{24,20},{28,16},{1,13},{... | collective-permute-start | bytes 405512 | tf_op jit(solution)/shard_map/ppermute | solution.py:597
  56.3 20.9 %collective-permute-start.18 = (bf16[528,512]{1,0:T(8,128)(2,1)S(1)}, bf16[528,512]{1,0:T(8,128)(2,1)S(1)}, u32[]{:S(2)}, u32[]{:S(2)}) collective-permute-start(bf16[528,512]{1,0:T(8,128)(2,1)S(1)} %get-tuple-element.57), channel_id=1, source_target_pairs={{0,2},{1,3},{2,0},{3,1},{4,6},{5,7},{6,4},{7,5},{8,10},{9,11},{10,... | collective-permute-start | bytes 1622024 | tf_op jit(solution)/shard_map/ppermute | solution.py:597
  57.8 21.5 %collective-permute-start.19 = (bf16[528,512]{1,0:T(8,128)(2,1)S(1)}, bf16[528,512]{1,0:T(8,128)(2,1)S(1)}, u32[]{:S(2)}, u32[]{:S(2)}) collective-permute-start(bf16[528,512]{1,0:T(8,128)(2,1)S(1)} %get-tuple-element.58), channel_id=1, source_target_pairs={{0,3},{1,2},{2,1},{3,0},{4,7},{5,6},{6,5},{7,4},{8,11},{9,10},{10,... | collective-permute-start | bytes 1622024 | tf_op jit(solution)/shard_map/ppermute | solution.py:597
  57.8 25.0 %collective-permute-start.15 = (bf16[528,512]{1,0:T(8,128)(2,1)S(1)}, bf16[528,512]{1,0:T(8,128)(2,1)S(1)}, u32[]{:S(2)}, u32[]{:S(2)}) collective-permute-start(bf16[528,512]{1,0:T(8,128)(2,1)S(1)} %get-tuple-element.54), channel_id=1, source_target_pairs={{0,1},{1,0},{2,3},{3,2},{4,5},{5,4},{6,7},{7,6},{8,9},{9,8},{10,11... | collective-permute-start | bytes 1622024 | tf_op jit(solution)/shard_map/ppermute | solution.py:597
  70.4 14.3 %collective-permute-start.12 = (bf16[16,4224]{1,0:T(8,128)(2,1)S(1)}, bf16[16,4224]{1,0:T(8,128)(2,1)S(1)}, u32[]{:S(2)}, u32[]{:S(2)}) collective-permute-start(bf16[16,4224]{1,0:T(8,128)(2,1)S(1)} %get-tuple-element.49), channel_id=1, source_target_pairs={{0,20},{4,16},{8,28},{12,24},{16,4},{20,0},{24,12},{28,8},{1,21},{... | collective-permute-start | bytes 405512 | tf_op jit(solution)/shard_map/ppermute | solution.py:597
  73.7 11.0 %collective-permute-start.13 = (bf16[16,4224]{1,0:T(8,128)(2,1)S(1)}, bf16[16,4224]{1,0:T(8,128)(2,1)S(1)}, u32[]{:S(2)}, u32[]{:S(2)}) collective-permute-start(bf16[16,4224]{1,0:T(8,128)(2,1)S(1)} %get-tuple-element.50), channel_id=1, source_target_pairs={{0,28},{4,24},{8,20},{12,16},{16,12},{20,8},{24,4},{28,0},{1,29},{... | collective-permute-start | bytes 405512 | tf_op jit(solution)/shard_map/ppermute | solution.py:597
  77.2 10.6 %collective-permute-start.3 = (bf16[16,4224]{1,0:T(8,128)(2,1)S(1)}, bf16[16,4224]{1,0:T(8,128)(2,1)S(1)}, u32[]{:S(2)}, u32[]{:S(2)}) collective-permute-start(bf16[16,4224]{1,0:T(8,128)(2,1)S(1)} %get-tuple-element.40), channel_id=1, source_target_pairs={{0,8},{4,12},{8,0},{12,4},{16,24},{20,28},{24,16},{28,20},{1,9},{5... | collective-permute-start | bytes 405512 | tf_op jit(solution)/shard_map/ppermute | solution.py:597
  79.3 17.4 %collective-permute-start.4 = (bf16[16,4224]{1,0:T(8,128)(2,1)S(1)}, bf16[16,4224]{1,0:T(8,128)(2,1)S(1)}, u32[]{:S(2)}, u32[]{:S(2)}) collective-permute-start(bf16[16,4224]{1,0:T(8,128)(2,1)S(1)} %get-tuple-element.41), channel_id=1, source_target_pairs={{0,16},{4,20},{8,24},{12,28},{16,0},{20,4},{24,8},{28,12},{1,17},{... | collective-permute-start | bytes 405512 | tf_op jit(solution)/shard_map/ppermute | solution.py:597
  82.8 13.9 %collective-permute-start.5 = (bf16[16,4224]{1,0:T(8,128)(2,1)S(1)}, bf16[16,4224]{1,0:T(8,128)(2,1)S(1)}, u32[]{:S(2)}, u32[]{:S(2)}) collective-permute-start(bf16[16,4224]{1,0:T(8,128)(2,1)S(1)} %get-tuple-element.42), channel_id=1, source_target_pairs={{0,24},{4,28},{8,16},{12,20},{16,8},{20,12},{24,0},{28,4},{1,25},{... | collective-permute-start | bytes 405512 | tf_op jit(solution)/shard_map/ppermute | solution.py:597
  (5 other events, 31.5 us)

commit v2 on v1

--- a/solution.py
+++ b/solution.py
@@ -324,9 +324,10 @@
     )
 
 
-def owner_body(w_uk, w_uv, latent, keys, *refs, arrays, capacity, sizes, scale):
+def owner_body(latent_far, w_uk, w_uv, keys, *refs, arrays, capacity, sizes, scale):
     pieces, outs = refs[:arrays], refs[arrays : 2 * arrays]
-    received, packed, query, both, result = refs[2 * arrays :]
+    received, packed, query, result, latent, sems = refs[2 * arrays :]
+    stream = Stream(latent_far, latent, sems, latent.shape[0], latent.shape[0])
     slots = received.shape[0]
     heads, width, wide = w_uk.shape
     values = w_uv.shape[2]
@@ -334,8 +335,6 @@
     top_rows = slots // shards
     base = heads * values
     rope_at = heads * width
-    both[:, 0:dims] = keys[...]
-    both[:, dims:] = keys[...]
     each = slots // arrays
     for k, piece in enumerate(pieces):
         received[k * each : (k + 1) * each, :] = piece[...].astype(received.dtype)
@@ -359,9 +358,8 @@
         block = max(2, min(heads, 512 // rows // 2 * 2))
         while heads % block:
             block -= 2
-        lane = iota((rows, 2 * dims), 1)
         column = iota((rows, LANES), 1)
-        chunk = 512
+        chunk = 256
         mine = pl.ds(pl.multiple_of(w * top_rows, top_rows), rows)
 
         def some_heads(step, _):
@@ -375,9 +373,9 @@
                 if j % 2 == 0:
                     pair_at = pl.multiple_of(rope_at + head * dims, LANES)
                     pair = packed[mine, pl.ds(pair_at, 2 * dims)]
-                keep = (lane < dims) if j % 2 == 0 else (lane >= dims)
-                query[at, wide:] = jnp.where(keep, pair, jnp.zeros_like(pair))
-
+                query[at, wide:] = pair[:, j % 2 * dims : (j % 2 + 1) * dims]
+            for k, copy in enumerate(stream.copies):
+                pl.when((w == k) & (step == 0))(copy.wait)
             q_latent = query[0 : block * rows, 0:wide]
             q_rotary = query[0 : block * rows, wide:]
             scores = []
@@ -386,7 +384,7 @@
                     q_latent, latent[w, t : t + chunk, :], NT, preferred_element_type=F32
                 )
                 scores.append(
-                    s + jnp.dot(q_rotary, both[w, :, t : t + chunk], preferred_element_type=F32)
+                    s + jnp.dot(q_rotary, keys[w, :, t : t + chunk], preferred_element_type=F32)
                 )
             highest = functools.reduce(
                 jnp.maximum, [jnp.max(s, axis=1, keepdims=True) for s in scores]
@@ -448,16 +446,18 @@
             owner_body, arrays=arrays, capacity=capacity, sizes=sizes, scale=scale
         ),
         [((each, heads * values + LANES), BF16)] * arrays,
-        20,
+        24,
         2 * heads * slots * tokens * (2 * wide + dims),
         scratch=[
             pltpu.VMEM((slots, received[0].shape[1]), BF16 if each % 16 == 0 else F32),
             pltpu.VMEM((slots, heads * (width + dims)), BF16),
-            pltpu.VMEM((max(512, 2 * top), wide + 2 * dims), BF16),
-            pltpu.VMEM((shards, 2 * dims, tokens), BF16),
+            pltpu.VMEM((max(512, 2 * top), wide + dims), BF16),
             pltpu.VMEM((slots, heads * values + LANES), BF16),
+            pltpu.VMEM(latent.shape, BF16),
+            pltpu.SemaphoreType.DMA((shards,)),
         ],
-        args=[w_uk, w_uv, latent, keys, *received],
+        far=[latent],
+        args=[w_uk, w_uv, keys, *received],
     )
 
 

time: 99.3 us -> 98.4 us (level)
  local copies, waits for them, and re-layouts: 4.41 us -> 2.21 us
  Pallas kernels: 37.3 us -> 38.3 us
    unnamed x18 -> x14, local copies, waits for them, and re-layouts: 4.41 us -> 2.21 us
    pallas_call x8, Pallas kernels: 37.3 us -> 38.3 us  [call(): pl.pallas_call(body, in_specs=[pl.BlockSpec(memory_space=space) for space...]
  transfers between devices with their start and end apart: 20 -> 20, of which waited for: 5 -> 6; matrix products, arithmetic and copies ran while one was open for 0% -> 0% of each run, Pallas kernels for 34% -> 36%
where the time goes in v2:
time: 98.4 us; the launch traced here: 97.6 us
  Pallas kernels  38.3 us (39%)
  starting transfers between devices  36.6 us (37%)
  waiting for transfers between devices  20.4 us (21%)
  local copies, waits for them, and re-layouts  2.21 us (2%)
    pallas_call x8, Pallas kernels, call(): pl.pallas_call(body, in_specs=[pl.BlockSpec(memory_space=space) for space...  38.3 us
    ppermute x20, starting transfers between devices, swap(): return lax.ppermute(x, axis, [(k, k ^ s) for k in range(size)])  36.6 us
    ppermute x20, waiting for transfers between devices, swap(): return lax.ppermute(x, axis, [(k, k ^ s) for k in range(size)])  20.4 us
    unnamed x14, local copies, waits for them, and re-layouts  2.21 us
  transfers between devices with their start and end apart: 20, of which 6 were waited for; matrix products, arithmetic and copies ran while one was open for 0% of the time, Pallas kernels for 36%

profile of v2, /device:TPU:0, one launch (start us, length us, event | category | flops | bytes accessed | tf_op | source)
XLA Modules:
  0.0 97.6 jit_solution(8917631914447914513)
XLA Ops:
  0.0 1.8 %shard_map.109 = (bf16[16,6272]{1,0:T(8,128)(2,1)S(1)}, bf16[16,6272]{1,0:T(8,128)(2,1)S(1)}, bf16[16,6272]{1,0:T(8,128)(2,1)S(1)}, bf16[16,6272]{1,0:T(8,128)(2...) custom-call(s32[1]{0:T(128)} %bitcast.me, ...), custom_call_target="tpu_custom_call" | custom-call | flops 102760448 | bytes 1048576 | tf_op jit(solution)/shard_map/pallas_call | solution.py:22
  1.8 3.0 %collective-permute-start.6 = (bf16[16,6272]{1,0:T(8,128)(2,1)S(1)}, bf16[16,6272]{1,0:T(8,128)(2,1)S(1)}, u32[]{:S(2)}, u32[]{:S(2)}) collective-permute-start(bf16[16,6272]{1,0:T(8,128)(2,1)S(1)} %get-tuple-element.43), channel_id=1, source_target_pairs={{0,4},{4,0},{8,12},{12,8},{16,20},{20,16},{24,28},{28,24},{1,5},{5... | collective-permute-start | bytes 602120 | tf_op jit(solution)/shard_map/ppermute | solution.py:597
  4.8 1.5 %collective-permute-start.7 = (bf16[16,6272]{1,0:T(8,128)(2,1)S(1)}, bf16[16,6272]{1,0:T(8,128)(2,1)S(1)}, u32[]{:S(2)}, u32[]{:S(2)}) collective-permute-start(bf16[16,6272]{1,0:T(8,128)(2,1)S(1)} %get-tuple-element.44), channel_id=1, source_target_pairs={{0,12},{4,8},{8,4},{12,0},{16,28},{20,24},{24,20},{28,16},{1,13},{... | collective-permute-start | bytes 602120 | tf_op jit(solution)/shard_map/ppermute | solution.py:597
  6.4 3.5 %collective-permute-start.8 = (bf16[16,6272]{1,0:T(8,128)(2,1)S(1)}, bf16[16,6272]{1,0:T(8,128)(2,1)S(1)}, u32[]{:S(2)}, u32[]{:S(2)}) collective-permute-start(bf16[16,6272]{1,0:T(8,128)(2,1)S(1)} %get-tuple-element.45), channel_id=1, source_target_pairs={{0,20},{4,16},{8,28},{12,24},{16,4},{20,0},{24,12},{28,8},{1,21},{... | collective-permute-start | bytes 602120 | tf_op jit(solution)/shard_map/ppermute | solution.py:597
  9.9 4.3 %shard_map.112 = (bf16[576,512]{1,0:T(8,128)(2,1)S(1)}, bf16[576,512]{1,0:T(8,128)(2,1)S(1)}, bf16[576,512]{1,0:T(8,128)(2,1)S(1)}, bf16[576,512]{1,0:T(8,128)(2,1)S(1)}) custom-call(s32[1]{0:T(128)} %bitcast.2.me, bf16[64,4096]{1,0:T(8,128)(2,1)} %nope_far.3, bf16[64,2048]{1,0:T(8,128)(2,1)} %rope_far.3, bf16[32,128,512]{2,1,0:T(8,128)(2,1)} %w_uk_far.1), custom_call_target="tpu_custom_call" | custom-call | flops 536870912 | bytes 1048576 | tf_op jit(solution)/shard_map/pallas_call | solution.py:22
  14.2 1.8 %collective-permute-start.16 = (bf16[576,512]{1,0:T(8,128)(2,1)S(1)}, bf16[576,512]{1,0:T(8,128)(2,1)S(1)}, u32[]{:S(2)}, u32[]{:S(2)}) collective-permute-start(bf16[576,512]{1,0:T(8,128)(2,1)S(1)} %get-tuple-element.55), channel_id=1, source_target_pairs={{0,2},{1,3},{2,0},{3,1},{4,6},{5,7},{6,4},{7,5},{8,10},{9,11},{10,... | collective-permute-start | bytes 1769480 | tf_op jit(solution)/shard_map/ppermute | solution.py:597
  15.9 1.8 %collective-permute-done.6.refs_0_ = bf16[16,6272]{1,0:T(8,128)(2,1)S(1)} collective-permute-done((bf16[16,6272]{1,0:T(8,128)(2,1)S(1)}, bf16[16,6272]{1,0:T(8,128)(2,1)S(1)}, u32[]{:S(2)}, u32[]{:S(2)}) %collective-permute-start.6) | collective-permute-done | bytes 200736 | tf_op jit(solution)/shard_map/ppermute | solution.py:597
  17.9 2.0 %collective-permute-start.14 = (bf16[576,512]{1,0:T(8,128)(2,1)S(1)}, bf16[576,512]{1,0:T(8,128)(2,1)S(1)}, u32[]{:S(2)}, u32[]{:S(2)}) collective-permute-start(bf16[576,512]{1,0:T(8,128)(2,1)S(1)} %get-tuple-element.52), channel_id=1, source_target_pairs={{0,1},{1,0},{2,3},{3,2},{4,5},{5,4},{6,7},{7,6},{8,9},{9,8},{10,11... | collective-permute-start | bytes 1769480 | tf_op jit(solution)/shard_map/ppermute | solution.py:597
  19.9 4.8 %collective-permute-done.8.refs_2_ = bf16[16,6272]{1,0:T(8,128)(2,1)S(1)} collective-permute-done((bf16[16,6272]{1,0:T(8,128)(2,1)S(1)}, bf16[16,6272]{1,0:T(8,128)(2,1)S(1)}, u32[]{:S(2)}, u32[]{:S(2)}) %collective-permute-start.8) | collective-permute-done | bytes 200736 | tf_op jit(solution)/shard_map/ppermute | solution.py:597
  24.7 4.4 %collective-permute-start.1 = (bf16[16,6272]{1,0:T(8,128)(2,1)S(1)}, bf16[16,6272]{1,0:T(8,128)(2,1)S(1)}, u32[]{:S(2)}, u32[]{:S(2)}) collective-permute-start(bf16[16,6272]{1,0:T(8,128)(2,1)S(1)} %get-tuple-element.37), channel_id=1, source_target_pairs={{0,16},{4,20},{8,24},{12,28},{16,0},{20,4},{24,8},{28,12},{1,17},{... | collective-permute-start | bytes 602120 | tf_op jit(solution)/shard_map/ppermute | solution.py:597
  29.1 2.2 %copy-done.1 = bf16[32,512,128]{2,1,0:T(8,128)(2,1)S(1)} copy-done((bf16[32,512,128]{2,1,0:T(8,128)(2,1)S(1)}, bf16[32,512,128]{2,1,0:T(8,128)(2,1)}, u32[]{:S(2)}) %copy-start.1) | copy-done | bytes 4194328
  31.3 10.7 %shard_map.111 = (bf16[16,4224]{1,0:T(8,128)(2,1)S(1)}, bf16[16,4224]{1,0:T(8,128)(2,1)S(1)}, bf16[16,4224]{1,0:T(8,128)(2,1)S(1)}, bf16[16,4224]{1,0:T(8,128)(2,1)S(1)}) custom-call(bf16[2,2048,512]{2,1,0:T(8,128)(2,1)} %latent_far.3, bf16[32,128,512]{2,1,0:T(8,128)(2,1)S(1)} %copy-done, bf16[32,512,128]{2,1,0:T(8,128)(2,1)S(1)} %copy-done.1, ...), custom_call_target="tpu_custom_call" | custom-call | flops 9126805504 | bytes 1048576 | tf_op jit(solution)/shard_map/pallas_call | solution.py:22
  43.2 5.8 %collective-permute-start.10 = (bf16[16,4224]{1,0:T(8,128)(2,1)S(1)}, bf16[16,4224]{1,0:T(8,128)(2,1)S(1)}, u32[]{:S(2)}, u32[]{:S(2)}) collective-permute-start(bf16[16,4224]{1,0:T(8,128)(2,1)S(1)} %get-tuple-element.47), channel_id=1, source_target_pairs={{0,4},{4,0},{8,12},{12,8},{16,20},{20,16},{24,28},{28,24},{1,5},{5... | collective-permute-start | bytes 405512 | tf_op jit(solution)/shard_map/ppermute | solution.py:597
  49.1 3.0 %shard_map.114 = (bf16[528,512]{1,0:T(8,128)(2,1)S(1)}, bf16[528,512]{1,0:T(8,128)(2,1)S(1)}) custom-call(s32[1]{0:T(128)} %bitcast.2.me, s32[64]{0:T(128)S(1)} %bitcast.4, bf16[16,256,512]{2,1,0:T(8,128)(2,1)S(1)} %copy-done.3, bf16[16,64,256]{2,1,0:T(8,128)(2,1)S(1)} %copy-done.4, bf16[576,512]{1,0:T(8,128)(2,1)S(1)} %collective-permute-done.16.refs_0_, ...), custom_call_target="tpu_custom_call" | custom-call | flops 2281701376 | bytes 1048576 | tf_op jit(solution)/shard_map/pallas_call | solution.py:22
  52.1 3.0 %shard_map.113 = (bf16[528,512]{1,0:T(8,128)(2,1)S(1)}, bf16[528,512]{1,0:T(8,128)(2,1)S(1)}) custom-call(s32[1]{0:T(128)} %bitcast.2.me, s32[64]{0:T(128)S(1)} %bitcast.5, bf16[16,256,512]{2,1,0:T(8,128)(2,1)S(1)} %copy-done.3, bf16[16,64,256]{2,1,0:T(8,128)(2,1)S(1)} %copy-done.4, bf16[576,512]{1,0:T(8,128)(2,1)S(1)} %get-tuple-element.51.refs_0_, ...), custom_call_target="tpu_custom_call" | custom-call | flops 2281701376 | bytes 1048576 | tf_op jit(solution)/shard_map/pallas_call | solution.py:22
  55.1 1.5 %collective-permute-start.18 = (bf16[528,512]{1,0:T(8,128)(2,1)S(1)}, bf16[528,512]{1,0:T(8,128)(2,1)S(1)}, u32[]{:S(2)}, u32[]{:S(2)}) collective-permute-start(bf16[528,512]{1,0:T(8,128)(2,1)S(1)} %get-tuple-element.57), channel_id=1, source_target_pairs={{0,2},{1,3},{2,0},{3,1},{4,6},{5,7},{6,4},{7,5},{8,10},{9,11},{10,... | collective-permute-start | bytes 1622024 | tf_op jit(solution)/shard_map/ppermute | solution.py:597
  57.2 12.3 %shard_map.110 = (bf16[16,4224]{1,0:T(8,128)(2,1)S(1)}, bf16[16,4224]{1,0:T(8,128)(2,1)S(1)}, bf16[16,4224]{1,0:T(8,128)(2,1)S(1)}, bf16[16,4224]{1,0:T(8,128)(2,1)S(1)}) custom-call(bf16[2,2048,512]{2,1,0:T(8,128)(2,1)} %latent_far.3, bf16[32,128,512]{2,1,0:T(8,128)(2,1)S(1)} %copy-done, bf16[32,512,128]{2,1,0:T(8,128)(2,1)S(1)} %copy-done.2, ...), custom_call_target="tpu_custom_call" | custom-call | flops 9126805504 | bytes 1048576 | tf_op jit(solution)/shard_map/pallas_call | solution.py:22
  69.6 3.2 %collective-permute-start.12 = (bf16[16,4224]{1,0:T(8,128)(2,1)S(1)}, bf16[16,4224]{1,0:T(8,128)(2,1)S(1)}, u32[]{:S(2)}, u32[]{:S(2)}) collective-permute-start(bf16[16,4224]{1,0:T(8,128)(2,1)S(1)} %get-tuple-element.49), channel_id=1, source_target_pairs={{0,20},{4,16},{8,28},{12,24},{16,4},{20,0},{24,12},{28,8},{1,21},{... | collective-permute-start | bytes 405512 | tf_op jit(solution)/shard_map/ppermute | solution.py:597
  72.8 3.8 %collective-permute-start.13 = (bf16[16,4224]{1,0:T(8,128)(2,1)S(1)}, bf16[16,4224]{1,0:T(8,128)(2,1)S(1)}, u32[]{:S(2)}, u32[]{:S(2)}) collective-permute-start(bf16[16,4224]{1,0:T(8,128)(2,1)S(1)} %get-tuple-element.50), channel_id=1, source_target_pairs={{0,28},{4,24},{8,20},{12,16},{16,12},{20,8},{24,4},{28,0},{1,29},{... | collective-permute-start | bytes 405512 | tf_op jit(solution)/shard_map/ppermute | solution.py:597
  78.1 3.5 %collective-permute-start.4 = (bf16[16,4224]{1,0:T(8,128)(2,1)S(1)}, bf16[16,4224]{1,0:T(8,128)(2,1)S(1)}, u32[]{:S(2)}, u32[]{:S(2)}) collective-permute-start(bf16[16,4224]{1,0:T(8,128)(2,1)S(1)} %get-tuple-element.41), channel_id=1, source_target_pairs={{0,16},{4,20},{8,24},{12,28},{16,0},{20,4},{24,8},{28,12},{1,17},{... | collective-permute-start | bytes 405512 | tf_op jit(solution)/shard_map/ppermute | solution.py:597
  82.0 1.6 %shard_map.115 = (bf16[64,4096]{1,0:T(8,128)(2,1)S(1)}, f32[64,128]{1,0:T(8,128)S(1)}) custom-call(s32[1]{0:T(128)} %bitcast.2.me, bf16[32,512,128]{2,1,0:T(8,128)(2,1)S(1)} %copy-done.2, bf16[528,512]{1,0:T(8,128)(2,1)S(1)} %get-tuple-element.53.refs_0_, bf16[528,512]{1,0:T(8,128)(2,1)S(1)} %collective-permute-done.15.refs_1_, ...), custom_call_target="tpu_custom_call" | custom-call | flops 536870912 | bytes 1048576 | tf_op jit(solution)/shard_map/pallas_call | solution.py:22
  84.0 3.1 %collective-permute-done.3.refs_3_ = bf16[16,4224]{1,0:T(8,128)(2,1)S(1)} collective-permute-done((bf16[16,4224]{1,0:T(8,128)(2,1)S(1)}, bf16[16,4224]{1,0:T(8,128)(2,1)S(1)}, u32[]{:S(2)}, u32[]{:S(2)}) %collective-permute-start.3) | collective-permute-done | bytes 135200 | tf_op jit(solution)/shard_map/ppermute | solution.py:597
  87.1 8.8 %collective-permute-done.4.refs_4_ = bf16[16,4224]{1,0:T(8,128)(2,1)S(1)} collective-permute-done((bf16[16,4224]{1,0:T(8,128)(2,1)S(1)}, bf16[16,4224]{1,0:T(8,128)(2,1)S(1)}, u32[]{:S(2)}, u32[]{:S(2)}) %collective-permute-start.4) | collective-permute-done | bytes 135200 | tf_op jit(solution)/shard_map/ppermute | solution.py:597
  95.9 1.8 %shard_map.116 = bf16[64,4096]{1,0:T(8,128)(2,1)} custom-call(bf16[64,64]{1,0:T(8,128)(2,1)S(1)} %get-tuple-element.33.refs_0_, bf16[64,64]{1,0:T(8,128)(2,1)S(1)} %get-tuple-element.34.refs_1_, bf16[16,4224]{1,0:T(8,128)(2,1)S(1)} %get-tuple-element.39.refs_2_, bf16[16,4224]{1,0:T(8,128)(2,1)S(1)} %collective-permute-done.3.refs_3_, ...), custom_call_target="tpu_custom_call" | custom-call | flops 33554432 | bytes 1048576 | tf_op jit(solution)/shard_map/pallas_call | solution.py:22
  (38 shorter events, 4.4 us)
Async XLA Ops:
  0.0 29.1 %copy-start.5 = (bf16[2,64,2048]{2,1,0:T(8,128)(2,1)S(1)}, bf16[2,64,2048]{2,1,0:T(8,128)(2,1)}, u32[]{:S(2)}) copy-start(bf16[2,64,2048]{2,1,0:T(8,128)(2,1)} %keys.5) | copy-start | bytes 1572868
  1.8 16.0 %collective-permute-start.6 = (bf16[16,6272]{1,0:T(8,128)(2,1)S(1)}, bf16[16,6272]{1,0:T(8,128)(2,1)S(1)}, u32[]{:S(2)}, u32[]{:S(2)}) collective-permute-start(bf16[16,6272]{1,0:T(8,128)(2,1)S(1)} %get-tuple-element.43), channel_id=1, source_target_pairs={{0,4},{4,0},{8,12},{12,8},{16,20},{20,16},{24,28},{28,24},{1,5},{5... | collective-permute-start | bytes 602120 | tf_op jit(solution)/shard_map/ppermute | solution.py:597
  4.8 13.1 %collective-permute-start.7 = (bf16[16,6272]{1,0:T(8,128)(2,1)S(1)}, bf16[16,6272]{1,0:T(8,128)(2,1)S(1)}, u32[]{:S(2)}, u32[]{:S(2)}) collective-permute-start(bf16[16,6272]{1,0:T(8,128)(2,1)S(1)} %get-tuple-element.44), channel_id=1, source_target_pairs={{0,12},{4,8},{8,4},{12,0},{16,28},{20,24},{24,20},{28,16},{1,13},{... | collective-permute-start | bytes 602120 | tf_op jit(solution)/shard_map/ppermute | solution.py:597
  6.4 18.3 %collective-permute-start.8 = (bf16[16,6272]{1,0:T(8,128)(2,1)S(1)}, bf16[16,6272]{1,0:T(8,128)(2,1)S(1)}, u32[]{:S(2)}, u32[]{:S(2)}) collective-permute-start(bf16[16,6272]{1,0:T(8,128)(2,1)S(1)} %get-tuple-element.45), channel_id=1, source_target_pairs={{0,20},{4,16},{8,28},{12,24},{16,4},{20,0},{24,12},{28,8},{1,21},{... | collective-permute-start | bytes 602120 | tf_op jit(solution)/shard_map/ppermute | solution.py:597
  9.9 14.8 %collective-permute-start.9 = (bf16[16,6272]{1,0:T(8,128)(2,1)S(1)}, bf16[16,6272]{1,0:T(8,128)(2,1)S(1)}, u32[]{:S(2)}, u32[]{:S(2)}) collective-permute-start(bf16[16,6272]{1,0:T(8,128)(2,1)S(1)} %get-tuple-element.46), channel_id=1, source_target_pairs={{0,28},{4,24},{8,20},{12,16},{16,12},{20,8},{24,4},{28,0},{1,29},{... | collective-permute-start | bytes 602120 | tf_op jit(solution)/shard_map/ppermute | solution.py:597
  9.9 19.2 %copy-start = (bf16[32,128,512]{2,1,0:T(8,128)(2,1)S(1)}, bf16[32,128,512]{2,1,0:T(8,128)(2,1)}, u32[]{:S(2)}) copy-start(bf16[32,128,512]{2,1,0:T(8,128)(2,1)} %w_uk_far.1) | copy-start | bytes 12582916
  14.2 27.8 %collective-permute-start.16 = (bf16[576,512]{1,0:T(8,128)(2,1)S(1)}, bf16[576,512]{1,0:T(8,128)(2,1)S(1)}, u32[]{:S(2)}, u32[]{:S(2)}) collective-permute-start(bf16[576,512]{1,0:T(8,128)(2,1)S(1)} %get-tuple-element.55), channel_id=1, source_target_pairs={{0,2},{1,3},{2,0},{3,1},{4,6},{5,7},{6,4},{7,5},{8,10},{9,11},{10,... | collective-permute-start | bytes 1769480 | tf_op jit(solution)/shard_map/ppermute | solution.py:597
  17.8 25.4 %collective-permute-start.17 = (bf16[576,512]{1,0:T(8,128)(2,1)S(1)}, bf16[576,512]{1,0:T(8,128)(2,1)S(1)}, u32[]{:S(2)}, u32[]{:S(2)}) collective-permute-start(bf16[576,512]{1,0:T(8,128)(2,1)S(1)} %get-tuple-element.56), channel_id=1, source_target_pairs={{0,3},{1,2},{2,1},{3,0},{4,7},{5,6},{6,5},{7,4},{8,11},{9,10},{10,... | collective-permute-start | bytes 1769480 | tf_op jit(solution)/shard_map/ppermute | solution.py:597
  17.9 34.1 %collective-permute-start.14 = (bf16[576,512]{1,0:T(8,128)(2,1)S(1)}, bf16[576,512]{1,0:T(8,128)(2,1)S(1)}, u32[]{:S(2)}, u32[]{:S(2)}) collective-permute-start(bf16[576,512]{1,0:T(8,128)(2,1)S(1)} %get-tuple-element.52), channel_id=1, source_target_pairs={{0,1},{1,0},{2,3},{3,2},{4,5},{5,4},{6,7},{7,6},{8,9},{9,8},{10,11... | collective-permute-start | bytes 1769480 | tf_op jit(solution)/shard_map/ppermute | solution.py:597
  24.7 30.4 %collective-permute-start = (bf16[16,6272]{1,0:T(8,128)(2,1)S(1)}, bf16[16,6272]{1,0:T(8,128)(2,1)S(1)}, u32[]{:S(2)}, u32[]{:S(2)}) collective-permute-start(bf16[16,6272]{1,0:T(8,128)(2,1)S(1)} %get-tuple-element.36), channel_id=1, source_target_pairs={{0,8},{4,12},{8,0},{12,4},{16,24},{20,28},{24,16},{28,20},{1,9},{5... | collective-permute-start | bytes 602120 | tf_op jit(solution)/shard_map/ppermute | solution.py:597
  24.7 31.9 %collective-permute-start.1 = (bf16[16,6272]{1,0:T(8,128)(2,1)S(1)}, bf16[16,6272]{1,0:T(8,128)(2,1)S(1)}, u32[]{:S(2)}, u32[]{:S(2)}) collective-permute-start(bf16[16,6272]{1,0:T(8,128)(2,1)S(1)} %get-tuple-element.37), channel_id=1, source_target_pairs={{0,16},{4,20},{8,24},{12,28},{16,0},{20,4},{24,8},{28,12},{1,17},{... | collective-permute-start | bytes 602120 | tf_op jit(solution)/shard_map/ppermute | solution.py:597
  31.3 17.8 %copy-start.4 = (bf16[16,64,256]{2,1,0:T(8,128)(2,1)S(1)}, bf16[16,64,256]{2,1,0:T(8,128)(2,1)}, u32[]{:S(2)}) copy-start(bf16[16,64,256]{2,1,0:T(8,128)(2,1)} %keys.7) | copy-start | bytes 1572868
  31.3 17.8 %copy-start.6 = (s32[1,64]{1,0:T(1,128)S(1)}, s32[1,64]{1,0:T(1,128)}, u32[]{:S(2)}) copy-start(s32[1,64]{1,0:T(1,128)} %param.19) | copy-start | bytes 772
  42.0 14.6 %collective-permute-start.2 = (bf16[16,6272]{1,0:T(8,128)(2,1)S(1)}, bf16[16,6272]{1,0:T(8,128)(2,1)S(1)}, u32[]{:S(2)}, u32[]{:S(2)}) collective-permute-start(bf16[16,6272]{1,0:T(8,128)(2,1)S(1)} %get-tuple-element.38), channel_id=1, source_target_pairs={{0,24},{4,28},{8,16},{12,20},{16,8},{20,12},{24,0},{28,4},{1,25},{... | collective-permute-start | bytes 602120 | tf_op jit(solution)/shard_map/ppermute | solution.py:597
  43.2 26.4 %collective-permute-start.10 = (bf16[16,4224]{1,0:T(8,128)(2,1)S(1)}, bf16[16,4224]{1,0:T(8,128)(2,1)S(1)}, u32[]{:S(2)}, u32[]{:S(2)}) collective-permute-start(bf16[16,4224]{1,0:T(8,128)(2,1)S(1)} %get-tuple-element.47), channel_id=1, source_target_pairs={{0,4},{4,0},{8,12},{12,8},{16,20},{20,16},{24,28},{28,24},{1,5},{5... | collective-permute-start | bytes 405512 | tf_op jit(solution)/shard_map/ppermute | solution.py:597
  52.0 20.8 %collective-permute-start.11 = (bf16[16,4224]{1,0:T(8,128)(2,1)S(1)}, bf16[16,4224]{1,0:T(8,128)(2,1)S(1)}, u32[]{:S(2)}, u32[]{:S(2)}) collective-permute-start(bf16[16,4224]{1,0:T(8,128)(2,1)S(1)} %get-tuple-element.48), channel_id=1, source_target_pairs={{0,12},{4,8},{8,4},{12,0},{16,28},{20,24},{24,20},{28,16},{1,13},{... | collective-permute-start | bytes 405512 | tf_op jit(solution)/shard_map/ppermute | solution.py:597
  55.1 21.6 %collective-permute-start.18 = (bf16[528,512]{1,0:T(8,128)(2,1)S(1)}, bf16[528,512]{1,0:T(8,128)(2,1)S(1)}, u32[]{:S(2)}, u32[]{:S(2)}) collective-permute-start(bf16[528,512]{1,0:T(8,128)(2,1)S(1)} %get-tuple-element.57), channel_id=1, source_target_pairs={{0,2},{1,3},{2,0},{3,1},{4,6},{5,7},{6,4},{7,5},{8,10},{9,11},{10,... | collective-permute-start | bytes 1622024 | tf_op jit(solution)/shard_map/ppermute | solution.py:597
  56.6 21.5 %collective-permute-start.19 = (bf16[528,512]{1,0:T(8,128)(2,1)S(1)}, bf16[528,512]{1,0:T(8,128)(2,1)S(1)}, u32[]{:S(2)}, u32[]{:S(2)}) collective-permute-start(bf16[528,512]{1,0:T(8,128)(2,1)S(1)} %get-tuple-element.58), channel_id=1, source_target_pairs={{0,3},{1,2},{2,1},{3,0},{4,7},{5,6},{6,5},{7,4},{8,11},{9,10},{10,... | collective-permute-start | bytes 1622024 | tf_op jit(solution)/shard_map/ppermute | solution.py:597
  56.6 25.0 %collective-permute-start.15 = (bf16[528,512]{1,0:T(8,128)(2,1)S(1)}, bf16[528,512]{1,0:T(8,128)(2,1)S(1)}, u32[]{:S(2)}, u32[]{:S(2)}) collective-permute-start(bf16[528,512]{1,0:T(8,128)(2,1)S(1)} %get-tuple-element.54), channel_id=1, source_target_pairs={{0,1},{1,0},{2,3},{3,2},{4,5},{5,4},{6,7},{7,6},{8,9},{9,8},{10,11... | collective-permute-start | bytes 1622024 | tf_op jit(solution)/shard_map/ppermute | solution.py:597
  69.6 14.0 %collective-permute-start.12 = (bf16[16,4224]{1,0:T(8,128)(2,1)S(1)}, bf16[16,4224]{1,0:T(8,128)(2,1)S(1)}, u32[]{:S(2)}, u32[]{:S(2)}) collective-permute-start(bf16[16,4224]{1,0:T(8,128)(2,1)S(1)} %get-tuple-element.49), channel_id=1, source_target_pairs={{0,20},{4,16},{8,28},{12,24},{16,4},{20,0},{24,12},{28,8},{1,21},{... | collective-permute-start | bytes 405512 | tf_op jit(solution)/shard_map/ppermute | solution.py:597
  72.8 11.2 %collective-permute-start.13 = (bf16[16,4224]{1,0:T(8,128)(2,1)S(1)}, bf16[16,4224]{1,0:T(8,128)(2,1)S(1)}, u32[]{:S(2)}, u32[]{:S(2)}) collective-permute-start(bf16[16,4224]{1,0:T(8,128)(2,1)S(1)} %get-tuple-element.50), channel_id=1, source_target_pairs={{0,28},{4,24},{8,20},{12,16},{16,12},{20,8},{24,4},{28,0},{1,29},{... | collective-permute-start | bytes 405512 | tf_op jit(solution)/shard_map/ppermute | solution.py:597
  76.7 10.4 %collective-permute-start.3 = (bf16[16,4224]{1,0:T(8,128)(2,1)S(1)}, bf16[16,4224]{1,0:T(8,128)(2,1)S(1)}, u32[]{:S(2)}, u32[]{:S(2)}) collective-permute-start(bf16[16,4224]{1,0:T(8,128)(2,1)S(1)} %get-tuple-element.40), channel_id=1, source_target_pairs={{0,8},{4,12},{8,0},{12,4},{16,24},{20,28},{24,16},{28,20},{1,9},{5... | collective-permute-start | bytes 405512 | tf_op jit(solution)/shard_map/ppermute | solution.py:597
  78.1 17.7 %collective-permute-start.4 = (bf16[16,4224]{1,0:T(8,128)(2,1)S(1)}, bf16[16,4224]{1,0:T(8,128)(2,1)S(1)}, u32[]{:S(2)}, u32[]{:S(2)}) collective-permute-start(bf16[16,4224]{1,0:T(8,128)(2,1)S(1)} %get-tuple-element.41), channel_id=1, source_target_pairs={{0,16},{4,20},{8,24},{12,28},{16,0},{20,4},{24,8},{28,12},{1,17},{... | collective-permute-start | bytes 405512 | tf_op jit(solution)/shard_map/ppermute | solution.py:597
  81.6 14.3 %collective-permute-start.5 = (bf16[16,4224]{1,0:T(8,128)(2,1)S(1)}, bf16[16,4224]{1,0:T(8,128)(2,1)S(1)}, u32[]{:S(2)}, u32[]{:S(2)}) collective-permute-start(bf16[16,4224]{1,0:T(8,128)(2,1)S(1)} %get-tuple-element.42), channel_id=1, source_target_pairs={{0,24},{4,28},{8,16},{12,20},{16,8},{20,12},{24,0},{28,4},{1,25},{... | collective-permute-start | bytes 405512 | tf_op jit(solution)/shard_map/ppermute | solution.py:597
  (3 other events, 25.1 us)
